TPU v7x, 32 devices: a whole 2x2x4 slice. The times are simulated.
32 devices in a mesh: ens: 2 (over y), space: 4 (over z), chan: 2 (over x), sub: 2 (over core).
Axes of the slice: x: 2, y: 2, z: 4, core: 2. Of those that a mesh axis runs over, the one named last changes fastest.
Arguments:
- node_state: bfloat16 [8192, 512], P(('ens', 'space'), ('chan', 'sub')), parts along dimension 0, may hold values from -6 to 6
- norm_gains: float32 [2, 512], replicated, may hold values from 0.25 to 1.75
- norm_shifts: float32 [2, 512], replicated, may hold values from -3 to 3
- query_weight: bfloat16 [512, 512], P(None, 'chan')
- key_weight: bfloat16 [512, 512], P(None, 'chan')
- value_weight: bfloat16 [512, 512], P(None, 'chan'), may hold values from -0.25 to 0.25
- out_weight: bfloat16 [512, 512], replicated, may hold values from -0.25 to 0.25
- ffn_in: bfloat16 [2048, 512], P('chan'), may hold values from -0.25 to 0.25
- ffn_out: bfloat16 [2048, 512], P('chan'), may hold values from -0.125 to 0.125
- live_counts: int32 [4], P('space'), may hold values from 512 to 1024, as said below
- send_rows: int32 [4, 2, 256], P('space'), may hold values from 0 to 1023, as said below
- tile_keys: int32 [32, 12], P('space'), may hold values from 0 to 11, as said below
- tile_bits: int32 [32, 12, 4, 128], P('space'), may hold values from -2147483648 to 2147483647, as said below
Outputs:
- updated: bfloat16 [8192, 512], P(('ens', 'space'), ('chan', 'sub')), parts along dimension 0
There are 2 independent parts, one for each index of `ens`. A program takes and returns all parts, laid end to end along the dimension named above; an argument that names none is the same for every part. Nothing has to cross between parts.
Inputs may be any that keep to these rules, and one draw needn't show every extreme that they name: Partition s has live nodes 0 to live_counts[s] - 1; the first and the last partition are full. send_rows[s, 0] lists nodes of partition s read by its lower neighbour, send_rows[s, 1] those read by its upper neighbour; all are live nodes, and entries may repeat. `tile_keys`: slot 0 of every block names the block itself (its index within the partition); other slots name blocks of the same partition (below 8), of the lower halo (from 8) or of the upper halo (from 10); the first partition names no lower halo and the last no upper halo. `tile_bits`: bit j of word w in column r of a slot says whether query r of the block may attend key 32 w + j of the slot's block (bit 31 is the sign bit); in slot 0 every query's own bit is set. Slots whose words are all zero carry no edges.
All inputs are finite; a program needn't handle non-finite values.
Results may differ from a plain program's by a relative error of at most 0.0095.
Values may be sent and summed in bfloat16 or wider, within the bound.
No kernel may reach another device: no remote copies, remote signals or barrier semaphores. Data moves between devices by JAX's collectives and lax.ppermute only.
A program may use at most 64 MiB of HBM per device.

v0:
```python
import math

import jax
import jax.numpy as jnp
from jax import lax
from jax.sharding import PartitionSpec as P

HD = 64


NORM_EPS = 1e-05
NEG_FILL = -1e30


def padded_2(array, sides, width):
    for axis, dim in sides:
        size, length = (lax.axis_size(axis), array.shape[dim])
        up = [(i, (i + 1) % size) for i in range(size - 1)]
        down = [(j, i) for i, j in up]
        last = lax.slice_in_dim(array, length - width, length, axis=dim)
        leading = lax.slice_in_dim(array, 0, width, axis=dim)
        before = lax.ppermute(last, axis, up)
        after = lax.ppermute(leading, axis, down)
        array = jnp.concatenate([before, array, after], axis=dim)
    return array


def normalize_rows(source, gain_row, shift_row):
    row_mean = jnp.mean(source, axis=-1, keepdims=True)
    spread = jnp.mean(source * source, axis=-1, keepdims=True) - row_mean * row_mean
    return (source - row_mean) * lax.rsqrt(spread + NORM_EPS) * gain_row + shift_row


def unpack_allowed(key_bits, key_ids, live_count, tile_size, blocks_own):
    shifts = jnp.arange(32, dtype=jnp.int32)
    expanded = jnp.right_shift(key_bits[..., None, :], shifts[:, None]) & 1
    lead_shape = key_bits.shape[:-2]
    expanded = expanded.reshape(lead_shape + (tile_size, tile_size))
    key_index = key_ids[..., None] * tile_size + jnp.arange(tile_size, dtype=jnp.int32)
    key_live = (key_ids[..., None] >= blocks_own) | (key_index < live_count)
    slot_count = key_ids.shape[-1]
    slot_first = jnp.arange(slot_count, dtype=jnp.int32)[:, None, None] == 0
    diagonal = (
        jnp.arange(tile_size, dtype=jnp.int32)[:, None]
        == jnp.arange(tile_size, dtype=jnp.int32)[None, :]
    )
    own_bit = slot_first & diagonal[None]
    return (expanded == 1) & (key_live[..., None] | own_bit)


def hidden_term(rows, in_piece, out_piece):
    hidden = jax.nn.gelu(
        lax.dot_general(
            rows, in_piece, (((1,), (1,)), ((), ())), preferred_element_type=jnp.float32
        )
    ).astype(jnp.bfloat16)
    return jnp.dot(hidden, out_piece, preferred_element_type=jnp.float32)


def on_device(
    node_state,
    norm_gains,
    norm_shifts,
    query_weight,
    key_weight,
    value_weight,
    out_weight,
    ffn_in,
    ffn_out,
    live_counts,
    send_rows,
    tile_keys,
    tile_bits,
):
    n_chan = lax.axis_size("chan")
    n_sub = lax.axis_size("sub")
    groups = n_chan * n_sub
    chan_at = lax.axis_index("chan")
    sub_at = lax.axis_index("sub")
    node_rank = chan_at * n_sub + sub_at
    node_count = node_state.shape[0]
    tile_size = tile_bits.shape[-1]
    word_count = tile_bits.shape[-2]
    slot_count = tile_keys.shape[1]
    blocks_own = tile_keys.shape[0]
    per_rank = node_count // groups
    head_cols = query_weight.shape[1]
    heads_here = head_cols // HD
    halo_rows = send_rows.shape[-1]
    live_count = live_counts[0]

    def own_half(source):
        step_rows = source.shape[0] // groups
        shaped = source.reshape((n_chan, n_sub, step_rows) + source.shape[1:])
        picked = lax.dynamic_index_in_dim(shaped, sub_at, 1, keepdims=False)
        return picked.reshape((n_chan * step_rows,) + source.shape[1:])

    node_rows = lax.all_to_all(node_state, ("chan", "sub"), split_axis=0, concat_axis=1, tiled=True)
    pair_weight = jnp.concatenate([key_weight, value_weight], axis=1)
    gathered = lax.all_gather(node_state, ("chan", "sub"), axis=1, tiled=True)
    normed = normalize_rows(gathered.astype(jnp.float32), norm_gains[0], norm_shifts[0]).astype(
        jnp.bfloat16
    )
    key_values = jnp.dot(normed, pair_weight, preferred_element_type=jnp.float32).astype(
        jnp.bfloat16
    )
    queries = jnp.dot(own_half(normed), query_weight, preferred_element_type=jnp.float32).astype(
        jnp.bfloat16
    )
    send_list = send_rows.reshape(2 * halo_rows)
    outgoing = jnp.take(key_values, send_list, axis=0)
    padded = padded_2(outgoing, (("space", 0),), halo_rows)
    extended = jnp.concatenate([key_values, padded[:halo_rows], padded[-halo_rows:]], axis=0)
    key_blocks = extended.reshape(-1, tile_size, 2 * head_cols)
    key_ids = own_half(tile_keys)
    key_bits = own_half(tile_bits)
    block_total = key_ids.shape[0]
    per_round = math.gcd(block_total, 4)
    rounds = block_total // per_round
    score_scale = 1.0 / math.sqrt(HD)

    def attend(inputs):
        q_part, id_part, bit_part = inputs
        chosen = key_blocks[id_part]
        keys_part = chosen[..., :head_cols].reshape(
            per_round, slot_count, tile_size, heads_here, HD
        )
        values_part = chosen[..., head_cols:].reshape(
            per_round, slot_count, tile_size, heads_here, HD
        )
        scores = (
            jnp.einsum("grhd,gtkhd->ghrtk", q_part, keys_part, preferred_element_type=jnp.float32)
            * score_scale
        )
        allowed = unpack_allowed(bit_part, id_part, live_count, tile_size, blocks_own)
        allowed = jnp.transpose(allowed, (0, 3, 1, 2))[:, None]
        masked = jnp.where(allowed, scores, NEG_FILL)
        row_max = jnp.max(masked, axis=(3, 4), keepdims=True)
        weights = jnp.where(allowed, jnp.exp(scores - row_max), 0.0)
        row_total = jnp.sum(weights, axis=(3, 4))
        mixed_heads = jnp.einsum(
            "ghrtk,gtkhd->grhd",
            weights.astype(jnp.bfloat16),
            values_part,
            preferred_element_type=jnp.float32,
        )
        mixed_heads = mixed_heads / jnp.transpose(row_total, (0, 2, 1))[..., None]
        return mixed_heads.astype(jnp.bfloat16).reshape(per_round * tile_size, head_cols)

    query_groups = queries.reshape(rounds, per_round, tile_size, heads_here, HD)
    attended = lax.map(
        attend,
        (
            query_groups,
            key_ids.reshape(rounds, per_round, slot_count),
            key_bits.reshape(rounds, per_round, slot_count, word_count, tile_size),
        ),
    )
    mixed_rows = jnp.dot(
        lax.all_to_all(
            attended.reshape(n_chan, per_rank, head_cols),
            "chan",
            split_axis=0,
            concat_axis=2,
            tiled=True,
        )[0],
        out_weight,
        preferred_element_type=jnp.float32,
    )
    after_attn = node_rows.astype(jnp.float32) + mixed_rows
    normed_two = normalize_rows(after_attn, norm_gains[1], norm_shifts[1]).astype(jnp.bfloat16)
    all_rows = lax.all_gather(normed_two, "chan", axis=0, tiled=True)
    update = lax.psum_scatter(
        hidden_term(all_rows, ffn_in, ffn_out).astype(jnp.bfloat16),
        "chan",
        scatter_dimension=0,
        tiled=True,
    ).astype(jnp.float32)
    position = node_rank * per_rank + jnp.arange(per_rank, dtype=jnp.int32)
    result = jnp.where((position < live_count)[:, None], after_attn + update, 0.0).astype(
        jnp.bfloat16
    )
    return lax.all_to_all(result, ("chan", "sub"), split_axis=1, concat_axis=0, tiled=True)


def solution(mesh):
    in_specs = (
        P(("ens", "space"), ("chan", "sub")),
        P(),
        P(),
        P(None, "chan"),
        P(None, "chan"),
        P(None, "chan"),
        P(),
        P("chan", None),
        P("chan", None),
        P("space"),
        P("space", None, None),
        P("space", None),
        P("space", None, None, None),
    )
    out_specs = P(("ens", "space"), ("chan", "sub"))
    return jax.shard_map(
        on_device, mesh=mesh, in_specs=in_specs, out_specs=out_specs, check_vma=False
    )
```

profile of v0, /device:TPU:0, one launch (start us, length us, event | category | flops | bytes accessed | tf_op | source)
XLA Modules:
  0.0 127.2 jit_solution(3869248447497856356)
XLA Ops:
  6.5 0.7 all-gather.2.cloned.1.call-update
  7.3 4.2 %all-to-all-start = ((bf16[4,256,128]{2,1,0:T(8,128)(2,1)}), bf16[4,256,128]{2,1,0:T(8,128)(2,1)}, u32[]{:S(2)}, u32[]{:S(2)}) async-start(bf16[4,256,128]{2,1,0:T(8,128)(2,1)} %bitcast.86), calls=%async_computation | async-start | bytes 524288 | tf_op jit(solution)/shard_map/all_to_all | solution.py:98
  14.4 0.9 constant_dynamic-slice_fusion.1
  15.6 1.2 fusion.10
  16.9 0.8 fusion.59
  17.7 0.8 fusion.60
  18.5 10.0 %all-gather.2.cloned.1.call-done = bf16[1024,512]{1,0:T(8,128)(2,1)} async-done(((bf16[1024,128]{1,0:T(8,128)(2,1)}), bf16[1024,512]{1,0:T(8,128)(2,1)}) %all-gather.2.cloned.1.call-update) | async-done | bytes 1048592 | tf_op jit(solution)/shard_map/all_gather | solution.py:100
  28.5 1.6 %convert_reduce_fusion = (f32[1024]{0:T(1024)S(1)}, f32[1024]{0:T(1024)S(1)}) fusion(bf16[1024,512]{1,0:T(8,128)(2,1)} %all-gather.2.cloned.1.call-done), kind=kLoop, calls=%fused_computation.17 | loop fusion | flops 2095104 | bytes 1056768 | tf_op jit(solution)/shard_map/reduce_sum | solution.py:29
  30.1 1.7 %fusion.14 = bf16[1024,512]{1,0:T(8,128)(2,1)S(1)} fusion(bf16[1024,512]{1,0:T(8,128)(2,1)} %all-gather.2.cloned.1.call-done, f32[512]{0:T(512)S(1)} %bitcast.103, f32[512]{0:T(512)S(1)} %bitcast.102, f32[1024]{0:T(1024)S(1)} %get-tuple-element.41, f32[1024]{0:T(1024)S(1)} %get-tuple-element.40), kind=kLoop, calls=%fused_computation.22 | loop fusion | flops 3145728 | bytes 2109440 | tf_op jit(solution)/shard_map/convert_element_type | solution.py:101
  31.8 1.0 copy-done.2
  32.8 0.7 convolution_convert_fusion
  33.5 2.0 %gather_fusion = bf16[512,512]{1,0:T(8,128)(2,1)S(1)} fusion(bf16[1024,512]{1,0:T(8,128)(2,1)S(1)} %convolution_convert_fusion, s32[1024]{0:T(1024)S(1)} %pad_clamp_fusion.1), kind=kCustom, calls=%fused_computation | custom fusion | bytes 1050624 | tf_op jit(solution)/shard_map/jit(_take)/gather | solution.py:111
  35.7 3.4 %collective-permute-start = (bf16[256,512]{1,0:T(8,128)(2,1)S(1)}, bf16[256,512]{1,0:T(8,128)(2,1)S(1)}, u32[]{:S(2)}, u32[]{:S(2)}) collective-permute-start(bf16[256,512]{1,0:T(8,128)(2,1)S(1)} %get-tuple-element.34), channel_id=1, source_target_pairs={{0,4},{4,8},{8,12},{1,5},{5,9},{9,13},{2,6},{6,10},{10,14},{3,7},{... | collective-permute-start | bytes 786440 | tf_op jit(solution)/shard_map/ppermute | solution.py:22
  39.1 1.3 %collective-permute-start.1 = (bf16[256,512]{1,0:T(8,128)(2,1)S(1)}, bf16[256,512]{1,0:T(8,128)(2,1)}, u32[]{:S(2)}, u32[]{:S(2)}) collective-permute-start(bf16[256,512]{1,0:T(8,128)(2,1)S(1)} %get-tuple-element.35), channel_id=1, source_target_pairs={{4,0},{8,4},{12,8},{5,1},{9,5},{13,9},{6,2},{10,6},{14,10},{7,3},{... | collective-permute-start | bytes 786440 | tf_op jit(solution)/shard_map/ppermute | solution.py:23
  40.4 1.1 constant_dynamic-slice_fusion
  41.8 1.1 reshape.235
  42.9 2.2 %collective-permute-done = bf16[256,512]{1,0:T(8,128)(2,1)S(1)} collective-permute-done((bf16[256,512]{1,0:T(8,128)(2,1)S(1)}, bf16[256,512]{1,0:T(8,128)(2,1)S(1)}, u32[]{:S(2)}, u32[]{:S(2)}) %collective-permute-start) | collective-permute-done | bytes 262176 | tf_op jit(solution)/shard_map/ppermute | solution.py:22
  45.7 3.5 %collective-permute-done.1 = bf16[256,512]{1,0:T(8,128)(2,1)} collective-permute-done((bf16[256,512]{1,0:T(8,128)(2,1)S(1)}, bf16[256,512]{1,0:T(8,128)(2,1)}, u32[]{:S(2)}, u32[]{:S(2)}) %collective-permute-start.1) | collective-permute-done | bytes 262176 | tf_op jit(solution)/shard_map/ppermute | solution.py:23
  49.3 1.5 %pad_maximum_fusion = bf16[1536,512]{1,0:T(8,128)(2,1)S(1)} fusion(bf16[256,512]{1,0:T(8,128)(2,1)} %collective-permute-done.1, bf16[256,512]{1,0:T(8,128)(2,1)} %copy-done.5, bf16[1024,512]{1,0:T(8,128)(2,1)} %copy-done.1), kind=kLoop, calls=%fused_computation.32 | loop fusion | flops 4718592 | bytes 3145728 | tf_op jit(solution)/shard_map/concatenate | solution.py:113
  50.8 5.0 %gather_fusion.1 = bf16[48,128,512]{2,1,0:T(8,128)(2,1)} fusion(bf16[12,128,512]{2,1,0:T(8,128)(2,1)S(1)} %bitcast.77, s32[1024]{0:T(1024)S(1)} %pad_clamp_fusion), kind=kCustom, calls=%fused_computation.1 | custom fusion | bytes 12583104 | tf_op jit(solution)/shard_map/while/body/eval_jaxpr/gather | solution.py:124
  55.7 8.6 %copy.29 = bf16[48,128,512]{1,2,0:T(8,128)(2,1)} copy(bf16[48,128,512]{2,1,0:T(8,128)(2,1)} %gather_fusion.1) | data formatting | bytes 12582912 | tf_op jit(solution)/shard_map/while/body/eval_jaxpr/gather | solution.py:124
  64.4 3.6 %fusion.57 = (bf16[4,12,128,256]{2,3,1,0:T(8,128)(2,1)S(1)}, bf16[4,12,128,256]{2,3,1,0:T(8,128)(2,1)S(1)}) fusion(bf16[4,12,128,512]{2,3,1,0:T(8,128)(2,1)} %bitcast.78), kind=kLoop, calls=%fused_computation.83 | loop fusion | bytes 12582912 | tf_op jit(solution)/shard_map/while/body/eval_jaxpr/slice | solution.py:128
  68.0 3.1 %select_reduce_fusion = (f32[4,4,128]{2,1,0:T(4,128)S(1)}, f32[4,4,128,12,128]{2,4,3,1,0:T(8,128)S(1)}) fusion(pred[4,128,12,128]{1,3,2,0:T(8,128)(4,1)S(1)} %bitcast.79, bf16[4,12,128,4,64]{2,4,3,1,0:T(8,128)(2,1)S(1)} %bitcast.83, bf16[4,128,4,64,1]{3,2,1,0,4:T(4,128)(2,1)S(1)} %bitcast.89), kind=kOutput, calls=%fused_computation.3 | convolution fusion | flops 412088320 | bytes 16785408 | tf_op jit(solution)/shard_map/while/body/eval_jaxpr/grhd,gtkhd->ghrtk/dot_general | solution.py:132
  71.1 2.8 %fusion = f32[4,4,128]{2,1,0:T(4,128)S(1)} fusion(f32[4,4,128,12,128]{2,4,3,1,0:T(8,128)S(1)} %get-tuple-element.45, f32[4,4,128]{2,1,0:T(4,128)S(1)} %get-tuple-element.44, pred[4,128,12,128]{1,3,2,0:T(8,128)(4,1)S(1)} %bitcast.80), kind=kLoop, calls=%fused_computation.4 | loop fusion | flops 12580864 | bytes 13385728 | tf_op jit(solution)/shard_map/while/body/eval_jaxpr/reduce_sum | solution.py:140
  73.9 3.4 %fusion.38 = bf16[4,128,4,64]{1,3,2,0:T(8,128)(2,1)S(1)} fusion(f32[4,4,128,12,128]{2,4,3,1,0:T(8,128)S(1)} %get-tuple-element.45, f32[4,4,128]{2,1,0:T(4,128)S(1)} %get-tuple-element.44, pred[4,128,12,128]{1,3,2,0:T(8,128)(4,1)S(1)} %bitcast.81, bf16[4,12,128,4,64]{2,4,3,1,0:T(8,128)(2,1)S(1)} %bitcast.82, f32[4,128,4]{1,2,0:T(4,128)S(1)} %bitcast.93), kind=kOutput, calls=%fused_computation.42 | convolution fusion | flops 415498240 | bytes 16793600 | tf_op jit(solution)/shard_map/while/body/eval_jaxpr/ghrtk,gtkhd->grhd/dot_general | solution.py:141
  77.8 7.6 %all_to_all.47 = bf16[2,256,256]{1,2,0:T(8,128)(2,1)S(1)} all-to-all(bf16[2,256,256]{1,2,0:T(8,128)(2,1)S(1)} %copy.36), channel_id=1, replica_groups=mesh['ens'=2,'space'=4,'chan'=2,'sub'=2] {'chan'}, dimensions={0} | all-to-all | bytes 524288 | tf_op jit(solution)/shard_map/all_to_all | solution.py:160
  85.4 1.4 %fusion.56 = (f32[256]{0:T(256)S(1)}, f32[256]{0:T(256)S(1)}, f32[256,512]{1,0:T(8,128)S(1)}) fusion(bf16[256,512]{0,1:T(8,128)(2,1)S(1)} %bitcast.88, bf16[512,512]{1,0:T(8,128)(2,1)S(1)} %copy-done.4, bf16[4,256,128]{2,1,0:T(8,128)(2,1)} %all-to-all-done), kind=kOutput, calls=%fused_computation.82 | convolution fusion | flops 134872576 | bytes 1574912 | tf_op jit(solution)/shard_map/dot_general | solution.py:159
  87.0 7.0 %all_gather.7 = bf16[512,512]{1,0:T(8,128)(2,1)S(1)} all-gather(bf16[256,512]{1,0:T(8,128)(2,1)S(1)} %add_convert_fusion), channel_id=1, replica_groups=mesh['ens'=2,'space'=4,'chan'=2,'sub'=2] {'chan'}, dimensions={0}, use_global_device_ids=true | all-gather | bytes 786432 | tf_op jit(solution)/shard_map/all_gather | solution.py:172
  94.0 2.3 %convolution_convert_fusion.1 = bf16[512,512]{1,0:T(8,128)(2,1)} fusion(bf16[1024,512]{1,0:T(8,128)(2,1)S(1)} %copy-done, bf16[512,512]{1,0:T(8,128)(2,1)S(1)} %all_gather.7, bf16[1024,512]{1,0:T(8,128)(2,1)S(1)} %copy-done.7), kind=kOutput, calls=%fused_computation.34 | convolution fusion | flops 1078722560 | bytes 3145728 | tf_op jit(solution)/shard_map/dot_general | solution.py:57
  96.3 13.9 %reduce-scatter.2.cloned.1.call-done = bf16[256,512]{1,0:T(8,128)(2,1)} async-done(((bf16[512,512]{1,0:T(8,128)(2,1)}), bf16[256,512]{1,0:T(8,128)(2,1)}) %reduce-scatter.2.cloned.1.call-update) | async-done | bytes 262160 | tf_op jit(solution)/shard_map/reduce_scatter | solution.py:173
  110.2 1.1 copy_bitcast_fusion
  111.2 8.4 %all_to_all.48 = bf16[256,4,128]{2,0,1:T(8,128)(2,1)S(1)} all-to-all(bf16[256,4,128]{2,0,1:T(8,128)(2,1)S(1)} %copy_bitcast_fusion), channel_id=1, replica_groups=mesh['ens'=2,'space'=4,'chan'=2,'sub'=2] {'chan','sub'}, dimensions={1} | all-to-all | bytes 524288 | tf_op jit(solution)/shard_map/all_to_all | solution.py:183
  (51 shorter events, 5.1 us)
Async XLA Ops:
  6.5 87.5 %copy-start = (bf16[1024,512]{1,0:T(8,128)(2,1)S(1)}, bf16[1024,512]{1,0:T(8,128)(2,1)}, u32[]{:S(2)}) copy-start(bf16[1024,512]{1,0:T(8,128)(2,1)} %param.21) | copy-start | bytes 3145732
  6.5 26.2 %copy-start.9 = (bf16[512,256]{1,0:T(8,128)(2,1)S(1)}, bf16[512,256]{1,0:T(8,128)(2,1)}, u32[]{:S(2)}) copy-start(bf16[512,256]{1,0:T(8,128)(2,1)} %param.17) | copy-start | bytes 786436
  6.5 26.2 %copy-start.8 = (bf16[512,256]{1,0:T(8,128)(2,1)S(1)}, bf16[512,256]{1,0:T(8,128)(2,1)}, u32[]{:S(2)}) copy-start(bf16[512,256]{1,0:T(8,128)(2,1)} %param.18) | copy-start | bytes 786436
  6.5 21.9 %all-gather.2.cloned.1.call-start = ((), (), s32[]{:S(2)}) async-start(), calls=%async_computation.4 | async-start | bytes 1310720 | tf_op jit(solution)/shard_map/all_gather | solution.py:100
  7.3 70.6 %all-to-all-start = ((bf16[4,256,128]{2,1,0:T(8,128)(2,1)}), bf16[4,256,128]{2,1,0:T(8,128)(2,1)}, u32[]{:S(2)}, u32[]{:S(2)}) async-start(bf16[4,256,128]{2,1,0:T(8,128)(2,1)} %bitcast.86), calls=%async_computation | async-start | bytes 524288 | tf_op jit(solution)/shard_map/all_to_all | solution.py:98
  11.5 98.7 %reduce-scatter.2.cloned.1.call-start = ((), (), s32[]{:S(2)}) async-start(), calls=%async_computation.5 | async-start | bytes 786432 | tf_op jit(solution)/shard_map/reduce_scatter | solution.py:173
  31.7 1.0 copy-start.2
  33.5 2.2 %copy-start.1 = (bf16[1024,512]{1,0:T(8,128)(2,1)}, bf16[1024,512]{1,0:T(8,128)(2,1)S(1)}, u32[]{:S(2)}) copy-start(bf16[1024,512]{1,0:T(8,128)(2,1)S(1)} %convolution_convert_fusion) | copy-start | bytes 3145732
  35.5 6.0 %copy-start.6 = (bf16[512,256]{1,0:T(8,128)(2,1)S(1)}, bf16[512,256]{1,0:T(8,128)(2,1)}, u32[]{:S(2)}) copy-start(bf16[512,256]{1,0:T(8,128)(2,1)} %param.16) | copy-start | bytes 786436
  35.7 9.3 %collective-permute-start = (bf16[256,512]{1,0:T(8,128)(2,1)S(1)}, bf16[256,512]{1,0:T(8,128)(2,1)S(1)}, u32[]{:S(2)}, u32[]{:S(2)}) collective-permute-start(bf16[256,512]{1,0:T(8,128)(2,1)S(1)} %get-tuple-element.34), channel_id=1, source_target_pairs={{0,4},{4,8},{8,12},{1,5},{5,9},{9,13},{2,6},{6,10},{10,14},{3,7},{... | collective-permute-start | bytes 786440 | tf_op jit(solution)/shard_map/ppermute | solution.py:22
  39.1 10.2 %collective-permute-start.1 = (bf16[256,512]{1,0:T(8,128)(2,1)S(1)}, bf16[256,512]{1,0:T(8,128)(2,1)}, u32[]{:S(2)}, u32[]{:S(2)}) collective-permute-start(bf16[256,512]{1,0:T(8,128)(2,1)S(1)} %get-tuple-element.35), channel_id=1, source_target_pairs={{4,0},{8,4},{12,8},{5,1},{9,5},{13,9},{6,2},{10,6},{14,10},{7,3},{... | collective-permute-start | bytes 786440 | tf_op jit(solution)/shard_map/ppermute | solution.py:23
  45.0 0.7 copy-start.5
  64.4 3.6 %copy-start.3 = (bf16[4,128,4,64]{3,2,1,0:T(4,128)(2,1)S(1)}, bf16[4,128,4,64]{3,2,1,0:T(4,128)(2,1)}, u32[]{:S(2)}) copy-start(bf16[4,128,4,64]{3,2,1,0:T(4,128)(2,1)} %reshape.235) | copy-start | bytes 786436
  73.9 11.5 %copy-start.4 = (bf16[512,512]{1,0:T(8,128)(2,1)S(1)}, bf16[512,512]{1,0:T(8,128)(2,1)}, u32[]{:S(2)}) copy-start(bf16[512,512]{1,0:T(8,128)(2,1)} %param.19) | copy-start | bytes 1572868
  77.4 16.6 %copy-start.7 = (bf16[1024,512]{1,0:T(8,128)(2,1)S(1)}, bf16[1024,512]{1,0:T(8,128)(2,1)}, u32[]{:S(2)}) copy-start(bf16[1024,512]{1,0:T(8,128)(2,1)} %param.20) | copy-start | bytes 3145732
Sparse Core Ops, SparseCore 0:
  8.9 19.5 all-gather.1
  96.4 13.7 reduce-scatter.1
where the time goes:
time: 128 us; the launch traced here: 127 us
  waiting for transfers between devices  30.3 us (24%)
  local copies, waits for them, and re-layouts  28.3 us (22%)
  blocking collectives  23 us (18%)
  between operations  14.3 us (11%)
  other arithmetic  11.2 us (9%)
  matrix products  11.2 us (9%)
  starting transfers between devices  8.95 us (7%)
    reduce_scatter x1, waiting for transfers between devices, on_device(): lax.psum_scatter(hidden_term(all_rows, ffn_in, ffn_out).astype(jnp.bfloat...  13.9 us
    gather x2, local copies, waits for them, and re-layouts, attend(): chosen = key_blocks[id_part]  13.6 us
    all_gather x1, waiting for transfers between devices, on_device(): gathered = lax.all_gather(node_state, ('chan', 'sub'), axis=1, tiled=True)  10 us
    all_to_all x1, blocking collectives, on_device(): lax.all_to_all(result, ('chan', 'sub'), split_axis=1, concat_axis=0, tile...  8.39 us
    all_to_all x1, blocking collectives, on_device(): lax.all_to_all(attended.reshape(n_chan, per_rank, head_cols), 'chan', spl...  7.56 us
    all_gather x1, blocking collectives, on_device(): all_rows = lax.all_gather(normed_two, 'chan', axis=0, tiled=True)  7.04 us
    all_to_all x1, starting transfers between devices, on_device(): lax.all_to_all(node_state, ('chan', 'sub'), split_axis=0, concat_axis=1,...  4.25 us
    unnamed x23, local copies, waits for them, and re-layouts  3.83 us
  transfers between devices with their start and end apart: 5, of which 4 were waited for; matrix products, arithmetic and copies ran while one was open for 34% of the time, Pallas kernels for 0%

commit v1 on v0

v1 whole, which is shorter than its diff:
```python
import functools
import math

import jax
import jax.numpy as jnp
from jax import lax
from jax.experimental import pallas as pl
from jax.experimental.pallas import tpu as pltpu
from jax.sharding import PartitionSpec as P

HD = 64


NORM_EPS = 1e-05
F32 = jnp.float32
BF16 = jnp.bfloat16
NT = (((1,), (1,)), ((), ()))
NN = (((1,), (0,)), ((), ()))


def dot(a, b, dims=NN):
    return lax.dot_general(a, b, dims, preferred_element_type=F32)


def normalize_rows(source, gain_row, shift_row):
    row_mean = jnp.mean(source, axis=-1, keepdims=True)
    spread = jnp.mean(source * source, axis=-1, keepdims=True) - row_mean * row_mean
    return (source - row_mean) * lax.rsqrt(spread + NORM_EPS) * gain_row + shift_row


def pick_body(list_ref, x_ref, up_ref, down_ref):
    rows = x_ref.shape[0]
    width = list_ref.shape[-1]
    source = x_ref[...]
    node = lax.broadcasted_iota(jnp.int32, (rows, width), 0)
    for at, out in ((1, up_ref), (0, down_ref)):
        hot = (node == list_ref[at : at + 1, :]).astype(F32).astype(BF16)
        out[...] = lax.dot_general(
            hot, source, (((0,), (0,)), ((), ())), preferred_element_type=F32
        ).astype(BF16)


def pick_rows(send_list, source):
    shape = jax.ShapeDtypeStruct((send_list.shape[1], source.shape[1]), source.dtype)
    return pl.pallas_call(pick_body, out_shape=(shape, shape), name="pick_rows")(send_list, source)


def project_body(chunk, pieces, meta_ref, *refs):
    mains, halos = refs[:pieces], refs[pieces : 2 * pieces]
    gain_ref, shift_ref, wq_ref, wk_ref, wvt_ref = refs[2 * pieces : 2 * pieces + 5]
    q_ref, k_ref, vt_ref, own_ref, xs_ref, ns_ref = refs[2 * pieces + 5 :]
    chan_at, sub_at = meta_ref[0], meta_ref[1]
    rows = mains[0].shape[0]
    cols = mains[0].shape[1]
    total = xs_ref.shape[0]
    for i in range(pieces):
        if pieces == 1:
            place = slice(None)
        else:
            chan_of = chan_at if i < 2 else 1 - chan_at
            sub_of = sub_at if i % 2 == 0 else 1 - sub_at
            place = pl.ds(pl.multiple_of((chan_of * 2 + sub_of) * cols, cols), cols)
        xs_ref[:rows, place] = mains[i][...]
        xs_ref[rows:, place] = halos[i][...]
    gain, shift = gain_ref[0:1, :], shift_ref[0:1, :]

    def step(j, carry):
        at = pl.ds(pl.multiple_of(j * chunk, chunk), chunk)
        normed = normalize_rows(xs_ref[at, :].astype(F32), gain, shift).astype(BF16)
        ns_ref[at, :] = normed
        k_ref[at, :] = dot(normed, wk_ref[...]).astype(BF16)
        vt_ref[:, at] = dot(wvt_ref[...], normed, NT).astype(BF16)
        return carry

    lax.fori_loop(0, total // chunk, step, 0)
    here = q_ref.shape[0]
    own = pl.ds(pl.multiple_of(sub_at * here, here), here)
    own_ref[...] = xs_ref[own, :]
    scale = 1.0 / math.sqrt(HD)
    q_ref[...] = (dot(ns_ref[own, :], wq_ref[...]).astype(BF16).astype(F32) * scale).astype(BF16)


def project(meta, mains, halos, gains, shifts, wq, wk, wvt, here):
    pieces = len(mains)
    total = mains[0].shape[0] + halos[0].shape[0]
    width = gains.shape[1]
    head_cols = wq.shape[1]
    vmem = pl.BlockSpec(memory_space=pltpu.VMEM)
    smem = pl.BlockSpec(memory_space=pltpu.SMEM)
    return pl.pallas_call(
        functools.partial(project_body, math.gcd(total, 256), pieces),
        out_shape=(
            jax.ShapeDtypeStruct((here, head_cols), BF16),
            jax.ShapeDtypeStruct((total, head_cols), BF16),
            jax.ShapeDtypeStruct((head_cols, total), BF16),
            jax.ShapeDtypeStruct((here, width), BF16),
        ),
        in_specs=[smem] + [vmem] * (2 * pieces + 5),
        out_specs=(vmem,) * 4,
        scratch_shapes=[pltpu.VMEM((total, width), BF16), pltpu.VMEM((total, width), BF16)],
        name="project",
    )(meta, *mains, *halos, gains, shifts, wq, wk, wvt)


def attend_body(
    blocks_own, meta_ref, live_ref, id_ref, q_ref, bit_ref, k_ref, vt_ref, out_ref, s_ref
):
    slot_count, word_count, tile = bit_ref.shape[1:]
    head_cols = q_ref.shape[1]
    heads = head_cols // HD
    block = meta_ref[1] * pl.num_programs(0) + pl.program_id(0)
    live = live_ref[0]
    q = q_ref[...]
    lane = lax.broadcasted_iota(jnp.int32, (tile, head_cols), 1)
    spread = jnp.concatenate(
        [jnp.where(lane // HD == h, q, jnp.zeros_like(q)) for h in range(heads)], axis=0
    )
    key_at = lax.broadcasted_iota(jnp.int32, (tile, tile), 0)
    query_at = lax.broadcasted_iota(jnp.int32, (tile, tile), 1)
    per_word = tile // word_count
    bit_at = lax.broadcasted_iota(jnp.int32, (per_word, tile), 0)
    peak = None
    starts = []
    for t in range(slot_count):
        key_id = id_ref[block, t]
        start = pl.multiple_of(key_id * tile, tile)
        starts.append(start)
        scores = dot(k_ref[pl.ds(start, tile), :], spread, NT)
        limit = jnp.where(key_id >= blocks_own, tile, live - key_id * tile)
        usable = key_at < limit
        if t == 0:
            usable = usable | (key_at == query_at)
        words = jnp.concatenate(
            [
                jnp.right_shift(
                    jnp.broadcast_to(bit_ref[0, t, w : w + 1, :], (per_word, tile)), bit_at
                )
                & 1
                for w in range(word_count)
            ],
            axis=0,
        )
        allowed = (words == 1) & usable
        for h in range(heads):
            part = jnp.where(allowed, scores[:, h * tile : (h + 1) * tile], -jnp.inf)
            s_ref[t * tile : (t + 1) * tile, h * tile : (h + 1) * tile] = part
        top = jnp.max(
            s_ref[t * tile : (t + 1) * tile, :].reshape(tile // 8, 8, heads * tile), axis=0
        )
        peak = top if peak is None else jnp.maximum(peak, top)
    peak = jnp.max(peak, axis=0, keepdims=True)
    group = math.gcd(heads, 2)
    per_dot = math.gcd(slot_count, 2)
    mixed = [None] * (heads // group)
    total = None
    for t in range(0, slot_count, per_dot):
        weights = jnp.exp(s_ref[t * tile : (t + per_dot) * tile, :] - peak)
        part = jnp.sum(weights.reshape(per_dot * tile // 8, 8, heads * tile), axis=0)
        total = part if total is None else total + part
        weights = weights.astype(BF16)
        for g in range(heads // group):
            values = jnp.concatenate(
                [
                    vt_ref[g * group * HD : (g + 1) * group * HD, pl.ds(starts[t + i], tile)]
                    for i in range(per_dot)
                ],
                axis=1,
            )
            add = dot(values, weights[:, g * group * tile : (g + 1) * group * tile])
            mixed[g] = add if mixed[g] is None else mixed[g] + add
    total = jnp.sum(total, axis=0, keepdims=True)
    pieces = []
    for h in range(heads):
        g, i = divmod(h, group)
        own = mixed[g][i * HD : (i + 1) * HD, i * tile : (i + 1) * tile]
        pieces.append(own / total[:, h * tile : (h + 1) * tile])
    out_ref[...] = jnp.concatenate(pieces, axis=0).T.astype(BF16)


def attend(meta, live_counts, tile_keys, queries, tile_bits, keys, values_t):
    blocks_own, slot_count, word_count, tile = tile_bits.shape
    here, head_cols = queries.shape
    total = keys.shape[0]
    count = here // tile
    heads = head_cols // HD
    return pl.pallas_call(
        functools.partial(attend_body, blocks_own),
        out_shape=jax.ShapeDtypeStruct((here, head_cols), BF16),
        grid_spec=pltpu.PrefetchScalarGridSpec(
            num_scalar_prefetch=3,
            grid=(count,),
            in_specs=[
                pl.BlockSpec((tile, head_cols), lambda i, m, n, k: (i, 0)),
                pl.BlockSpec(
                    (1, slot_count, word_count, tile),
                    lambda i, m, n, k: (m[1] * count + i, 0, 0, 0),
                ),
                pl.BlockSpec((total, head_cols), lambda i, m, n, k: (0, 0)),
                pl.BlockSpec((head_cols, total), lambda i, m, n, k: (0, 0)),
            ],
            out_specs=pl.BlockSpec((tile, head_cols), lambda i, m, n, k: (i, 0)),
            scratch_shapes=[pltpu.VMEM((slot_count * tile, heads * tile), F32)],
        ),
        name="attend",
    )(meta, live_counts, tile_keys, queries, tile_bits, keys, values_t)


def feed_body(chunk, paired, meta_ref, *refs):
    count = 2 if paired else 1
    mixed = refs[:count]
    x_ref, wo_ref, gain_ref, shift_ref, in_ref, out_w_ref, send_ref, keep_ref = refs[count:]
    chan_at = meta_ref[0]
    here, width = x_ref.shape
    gain, shift = gain_ref[1:2, :], shift_ref[1:2, :]

    def step(j, carry):
        at = pl.ds(pl.multiple_of(j * chunk, chunk), chunk)
        after = x_ref[at, :].astype(F32)
        for i in range(count):
            cols = mixed[i].shape[1]
            if paired:
                chan_of = chan_at if i == 0 else 1 - chan_at
                weight = wo_ref[pl.ds(pl.multiple_of(chan_of * cols, cols), cols), :]
            else:
                weight = wo_ref[...]
            after = after + dot(mixed[i][at, :], weight)
        normed = normalize_rows(after, gain, shift).astype(BF16)
        hidden = jax.nn.gelu(dot(normed, in_ref[...], NT)).astype(BF16)
        update = dot(hidden, out_w_ref[...])
        if paired:
            half = width // 2
            first = chan_at == 0
            send_ref[at, :] = jnp.where(first, update[:, half:], update[:, :half]).astype(BF16)
            both = after + update
            keep_ref[at, :] = jnp.where(first, both[:, :half], both[:, half:])
        else:
            send_ref[at, :] = update.astype(BF16)
            keep_ref[at, :] = after
        return carry

    lax.fori_loop(0, here // chunk, step, 0)


def feed(meta, mixed, own_x, out_weight, gains, shifts, ffn_in, ffn_out):
    paired = len(mixed) == 2
    here, width = own_x.shape
    cols = width // 2 if paired else width
    vmem = pl.BlockSpec(memory_space=pltpu.VMEM)
    smem = pl.BlockSpec(memory_space=pltpu.SMEM)
    return pl.pallas_call(
        functools.partial(feed_body, math.gcd(here, 256), paired),
        out_shape=(
            jax.ShapeDtypeStruct((here, cols), BF16),
            jax.ShapeDtypeStruct((here, cols), F32),
        ),
        in_specs=[smem] + [vmem] * (len(mixed) + 6),
        out_specs=(vmem, vmem),
        name="feed",
    )(meta, *mixed, own_x, out_weight, gains, shifts, ffn_in, ffn_out)


def swap(array, axis):
    return lax.ppermute(array, axis, [(0, 1), (1, 0)])


def on_device(
    node_state,
    norm_gains,
    norm_shifts,
    query_weight,
    key_weight,
    value_weight,
    out_weight,
    ffn_in,
    ffn_out,
    live_counts,
    send_rows,
    tile_keys,
    tile_bits,
):
    n_chan = lax.axis_size("chan")
    n_sub = lax.axis_size("sub")
    n_space = lax.axis_size("space")
    paired = n_chan == 2 and n_sub == 2
    chan_at = lax.axis_index("chan")
    sub_at = lax.axis_index("sub")
    node_count, local_cols = node_state.shape
    here = node_count // n_sub
    meta = jnp.stack([chan_at, sub_at]).astype(jnp.int32)

    up = [(i, i + 1) for i in range(n_space - 1)]
    down = [(i + 1, i) for i in range(n_space - 1)]
    if paired:
        across = swap(node_state, "chan")
    upward, downward = pick_rows(send_rows[0], node_state)
    lower = lax.ppermute(upward, "space", up)
    upper = lax.ppermute(downward, "space", down)
    halo = jnp.concatenate([lower, upper], axis=0)
    if paired:
        halo_across = swap(halo, "chan")
        mains = [node_state, swap(node_state, "sub"), across, swap(across, "sub")]
        halos = [halo, swap(halo, "sub"), halo_across, swap(halo_across, "sub")]
    else:
        mains = [lax.all_gather(node_state, ("chan", "sub"), axis=1, tiled=True)]
        halos = [lax.all_gather(halo, ("chan", "sub"), axis=1, tiled=True)]
    queries, keys, values_t, own_x = project(
        meta, mains, halos, norm_gains, norm_shifts, query_weight, key_weight, value_weight.T, here
    )
    attended = attend(meta, live_counts, tile_keys, queries, tile_bits, keys, values_t)
    if paired:
        mixed = [attended, swap(attended, "chan")]
    else:
        mixed = [lax.all_gather(attended, "chan", axis=1, tiled=True)]
    send, keep = feed(meta, mixed, own_x, out_weight, norm_gains, norm_shifts, ffn_in, ffn_out)
    if paired:
        total = keep + swap(send, "chan").astype(F32)
    else:
        width = keep.shape[1] // n_chan
        kept = lax.dynamic_slice_in_dim(keep, chan_at * width, width, 1)
        total = kept + lax.psum_scatter(send, "chan", scatter_dimension=1, tiled=True).astype(F32)
    position = sub_at * here + jnp.arange(here, dtype=jnp.int32)
    result = jnp.where((position < live_counts[0])[:, None], total, 0.0).astype(BF16)
    if paired:
        first = sub_at == 0
        mine = jnp.where(first, result[:, :local_cols], result[:, local_cols:])
        theirs = swap(jnp.where(first, result[:, local_cols:], result[:, :local_cols]), "sub")
        return jnp.concatenate(
            [jnp.where(first, mine, theirs), jnp.where(first, theirs, mine)], axis=0
        )
    return lax.all_to_all(result, "sub", split_axis=1, concat_axis=0, tiled=True)


def solution(mesh):
    in_specs = (
        P(("ens", "space"), ("chan", "sub")),
        P(),
        P(),
        P(None, "chan"),
        P(None, "chan"),
        P(None, "chan"),
        P(),
        P("chan", None),
        P("chan", None),
        P("space"),
        P("space", None, None),
        P("space", None),
        P("space", None, None, None),
    )
    out_specs = P(("ens", "space"), ("chan", "sub"))
    return jax.shard_map(
        on_device, mesh=mesh, in_specs=in_specs, out_specs=out_specs, check_vma=False
    )
```

time: 128 us -> 67.4 us (0.53)
  local copies, waits for them, and re-layouts: 28.3 us -> 2.43 us
  Pallas kernels: 0 us -> 24.7 us
  blocking collectives: 23 us -> 0 us
  between operations: 14.3 us -> 0.8 us
  matrix products: 11.2 us -> 0 us
  other arithmetic: 11.2 us -> 2.6 us
  waiting for transfers between devices: 30.3 us -> 26.6 us
    pallas_call x0 -> x4, Pallas kernels: none -> 24.7 us  [the longest x1 11.5 us: attend(): pl.pallas_call(functools.partial(attend_body, blocks_own), out_shape=jax....]
    ppermute x2 -> x11, waiting for transfers between devices: 5.7 us -> 26.6 us  [the longest x9 21.3 us: swap(): return lax.ppermute(array, axis, [(0, 1), (1, 0)])]
    all_to_all x2 -> x0, blocking collectives: 16 us -> none  [the longest x1 8.39 us: on_device(): lax.all_to_all(result, ('chan', 'sub'), split_axis=1, concat_axis=0, tile...]
    gather x3 -> x0, local copies, waits for them, and re-layouts: 15.6 us -> none  [the longest x2 13.6 us: attend(): chosen = key_blocks[id_part]]
    reduce_scatter x1 -> x0, waiting for transfers between devices: 13.9 us -> none  [on_device(): lax.psum_scatter(hidden_term(all_rows, ffn_in, ffn_out).astype(jnp.bfloat...]
    dot_general x6 -> x0, matrix products: 11.2 us -> none  [the longest x1 3.42 us: attend(): jnp.einsum('ghrtk,gtkhd->grhd', weights.astype(jnp.bfloat16), values_part...]
    all_gather x1 -> x0, waiting for transfers between devices: 10 us -> none  [on_device(): gathered = lax.all_gather(node_state, ('chan', 'sub'), axis=1, tiled=True)]
    all_gather x1 -> x0, blocking collectives: 7.04 us -> none  [on_device(): all_rows = lax.all_gather(normed_two, 'chan', axis=0, tiled=True)]
  transfers between devices with their start and end apart: 5 -> 11, of which waited for: 4 -> 5; matrix products, arithmetic and copies ran while one was open for 34% -> 2% of each run, Pallas kernels for 0% -> 0%
where the time goes in v1:
time: 67.4 us; the launch traced here: 67.1 us
  waiting for transfers between devices  26.6 us (39%)
  Pallas kernels  24.7 us (37%)
  starting transfers between devices  10 us (15%)
  other arithmetic  2.6 us (4%)
  local copies, waits for them, and re-layouts  2.43 us (4%)
  between operations  0.8 us (1%)
    ppermute x9, waiting for transfers between devices, swap(): return lax.ppermute(array, axis, [(0, 1), (1, 0)])  21.3 us
    pallas_call x1, Pallas kernels, attend(): pl.pallas_call(functools.partial(attend_body, blocks_own), out_shape=jax....  11.5 us
    pallas_call x1, Pallas kernels, project(): pl.pallas_call(functools.partial(project_body, math.gcd(total, 256), piec...  5.73 us
    pallas_call x1, Pallas kernels, feed(): pl.pallas_call(functools.partial(feed_body, math.gcd(here, 256), paired),...  5.32 us
    ppermute x1, waiting for transfers between devices, on_device(): upper = lax.ppermute(downward, 'space', down)  5.28 us
    ppermute x1, starting transfers between devices, on_device(): lower = lax.ppermute(upward, 'space', up)  4.95 us
    ppermute x9, starting transfers between devices, swap(): return lax.ppermute(array, axis, [(0, 1), (1, 0)])  3.82 us
    unnamed x22, local copies, waits for them, and re-layouts  2.42 us
  transfers between devices with their start and end apart: 11, of which 5 were waited for; matrix products, arithmetic and copies ran while one was open for 2% of the time, Pallas kernels for 0%

profile of v1, /device:TPU:0, one launch (start us, length us, event | category | flops | bytes accessed | tf_op | source)
XLA Modules:
  0.0 67.1 jit_solution(5552638960901658418)
XLA Ops:
  0.0 2.1 %pick_rows.1 = (bf16[256,128]{1,0:T(8,128)(2,1)}, bf16[256,128]{1,0:T(8,128)(2,1)}) custom-call(s32[2,256]{1,0:T(2,128)} %bitcast.7, bf16[1024,128]{1,0:T(8,128)(2,1)} %refs_0_.1), custom_call_target="tpu_custom_call" | custom-call | tf_op jit(solution)/shard_map/pick_rows/pallas_call | solution.py:45
  2.1 4.9 %collective-permute-start.3 = (bf16[256,128]{1,0:T(8,128)(2,1)}, bf16[256,128]{1,0:T(8,128)(2,1)S(1)}, u32[]{:S(2)}, u32[]{:S(2)}) collective-permute-start(bf16[256,128]{1,0:T(8,128)(2,1)} %get-tuple-element.13), channel_id=1, source_target_pairs={{0,4},{4,8},{8,12},{1,5},{5,9},{9,13},{2,6},{6,10},{10,14},{3,7},{... | collective-permute-start | bytes 196616 | tf_op jit(solution)/shard_map/ppermute | solution.py:296
  7.1 1.6 %collective-permute-start.1 = (bf16[1024,128]{1,0:T(8,128)(2,1)S(1)}, bf16[1024,128]{1,0:T(8,128)(2,1)S(1)}, u32[]{:S(2)}, u32[]{:S(2)}) collective-permute-start(bf16[1024,128]{1,0:T(8,128)(2,1)S(1)} %copy-done), channel_id=1, source_target_pairs={{0,2},{2,0},{1,3},{3,1},{4,6},{6,4},{5,7},{7,5},{8,10},{10,8},{9,1... | collective-permute-start | bytes 786440 | tf_op jit(solution)/shard_map/ppermute | solution.py:263
  8.7 0.0 collective-permute-start
  8.7 1.3 %collective-permute-start.4 = (bf16[256,128]{1,0:T(8,128)(2,1)}, bf16[256,128]{1,0:T(8,128)(2,1)S(1)}, u32[]{:S(2)}, u32[]{:S(2)}) collective-permute-start(bf16[256,128]{1,0:T(8,128)(2,1)} %get-tuple-element.14), channel_id=1, source_target_pairs={{4,0},{8,4},{12,8},{5,1},{9,5},{13,9},{6,2},{10,6},{14,10},{7,3},{... | collective-permute-start | bytes 196616 | tf_op jit(solution)/shard_map/ppermute | solution.py:297
  10.0 0.0 collective-permute-done.3
  10.0 5.3 %collective-permute-done.4 = bf16[256,128]{1,0:T(8,128)(2,1)S(1)} collective-permute-done((bf16[256,128]{1,0:T(8,128)(2,1)}, bf16[256,128]{1,0:T(8,128)(2,1)S(1)}, u32[]{:S(2)}, u32[]{:S(2)}) %collective-permute-start.4) | collective-permute-done | bytes 65568 | tf_op jit(solution)/shard_map/ppermute | solution.py:297
  15.3 0.6 collective-permute-start.6
  15.9 0.5 collective-permute-start.5
  16.4 4.0 %collective-permute-done.6.refs_6_ = bf16[512,128]{1,0:T(8,128)(2,1)S(1)} collective-permute-done((bf16[512,128]{1,0:T(8,128)(2,1)S(1)}, bf16[512,128]{1,0:T(8,128)(2,1)S(1)}, u32[]{:S(2)}, u32[]{:S(2)}) %collective-permute-start.6) | collective-permute-done | bytes 131104 | tf_op jit(solution)/shard_map/ppermute | solution.py:263
  20.4 0.0 collective-permute-start.7
  20.4 0.8 %copy.14 = bf16[512,256]{0,1:T(8,128)(2,1)} copy(bf16[512,256]{1,0:T(8,128)(2,1)S(1)} %copy-done.2) | data formatting | bytes 524288 | tf_op args[5]
  21.9 0.7 pad_add_fusion.meta_ref
  22.6 0.0 collective-permute-done.refs_1_
  22.6 0.0 copy-start.4
  22.6 0.0 collective-permute-done.2.refs_3_
  22.6 0.6 copy-done.8
  23.2 0.1 copy-done.4
  23.3 0.0 copy-done.9
  23.4 0.1 copy-done.5
  23.5 5.7 %project.1 = (bf16[512,256]{1,0:T(8,128)(2,1)}, bf16[1536,256]{1,0:T(8,128)(2,1)}, bf16[256,1536]{1,0:T(8,128)(2,1)}, bf16[512,512]{1,0:T(8,128)(2,1)}) custom-call(s32[2]{0:T(128)} %pad_add_fusion.meta_ref, bf16[1024,128]{1,0:T(8,128)(2,1)} %refs_0_.1, bf16[1024,128]{1,0:T(8,128)(2,1)} %copy-done.4, bf16[1024,128]{1,0:T(8,128)(2,1)} %copy-done.3, ...), custom_call_target="tpu_custom_call" | custom-call | tf_op jit(solution)/shard_map/project/pallas_call | solution.py:90
  29.2 11.5 %attend.1.refs_0_ = bf16[512,256]{1,0:T(8,128)(2,1)} custom-call(s32[2]{0:T(128)} %pad_add_fusion.meta_ref, s32[1]{0:T(128)} %copy.16.live_ref, s32[8,12]{1,0:T(8,128)} %id_ref.1, bf16[512,256]{1,0:T(8,128)(2,1)} %get-tuple-element.15.q_ref, s32[8,12,4,128]{3,2,1,0:T(4,128)} %bit_ref.1, bf16[1536,256]{1,0:T(8,128)(2,1)} %get-tuple-element.16.k_ref, ...), custom_call_target="tpu_custom_call" | custom-call | tf_op jit(solution)/shard_map/attend/pallas_call | solution.py:186
  40.7 0.5 collective-permute-start.8
  41.2 8.4 %collective-permute-done.8.refs_1_ = bf16[512,256]{1,0:T(8,128)(2,1)S(1)} collective-permute-done((bf16[512,256]{1,0:T(8,128)(2,1)}, bf16[512,256]{1,0:T(8,128)(2,1)S(1)}, u32[]{:S(2)}, u32[]{:S(2)}) %collective-permute-start.8) | collective-permute-done | bytes 262176 | tf_op jit(solution)/shard_map/ppermute | solution.py:263
  49.6 0.7 %copy-done.6 = bf16[512,256]{1,0:T(8,128)(2,1)} copy-done((bf16[512,256]{1,0:T(8,128)(2,1)}, bf16[512,256]{1,0:T(8,128)(2,1)S(1)}, u32[]{:S(2)}) %copy-start.6) | copy-done | bytes 262168
  50.3 5.3 %feed.1 = (bf16[512,256]{1,0:T(8,128)(2,1)}, f32[512,256]{1,0:T(8,128)}) custom-call(s32[2]{0:T(128)} %pad_add_fusion.meta_ref, bf16[512,256]{1,0:T(8,128)(2,1)} %attend.1.refs_0_, bf16[512,256]{1,0:T(8,128)(2,1)} %copy-done.6, bf16[512,512]{1,0:T(8,128)(2,1)} %get-tuple-element.18.refs_2_, bf16[512,512]{1,0:T(8,128)(2,1)} %refs_3_.1, f32[2,512]{1,0:T(2,128)} %refs_4_.1, ...), custom_call_target="tpu_custom_call" | custom-call | tf_op jit(solution)/shard_map/feed/pallas_call | solution.py:250
  55.7 0.5 collective-permute-start.9
  56.2 7.5 %collective-permute-done.9 = bf16[512,256]{1,0:T(8,128)(2,1)S(1)} collective-permute-done((bf16[512,256]{1,0:T(8,128)(2,1)}, bf16[512,256]{1,0:T(8,128)(2,1)S(1)}, u32[]{:S(2)}, u32[]{:S(2)}) %collective-permute-start.9) | collective-permute-done | bytes 262176 | tf_op jit(solution)/shard_map/ppermute | solution.py:263
  63.7 1.2 %select_convert_fusion = bf16[512,256]{1,0:T(8,128)(2,1)S(1)} fusion(f32[512,256]{1,0:T(8,128)} %get-tuple-element.19, bf16[512,256]{1,0:T(8,128)(2,1)S(1)} %collective-permute-done.9, pred[512]{0:T(512)(128)(4,1)S(1)} %add_compare_fusion), kind=kLoop, calls=%fused_computation | loop fusion | flops 524288 | bytes 1049088 | tf_op jit(solution)/shard_map/convert_element_type | solution.py:322
  64.9 0.1 collective-permute-start.10
  65.0 1.3 %collective-permute-done.10 = bf16[512,128]{1,0:T(8,128)(2,1)S(1)} collective-permute-done((bf16[512,128]{1,0:T(8,128)(2,1)S(1)}, bf16[512,128]{1,0:T(8,128)(2,1)S(1)}, u32[]{:S(2)}, u32[]{:S(2)}) %collective-permute-start.10) | collective-permute-done | bytes 131104 | tf_op jit(solution)/shard_map/ppermute | solution.py:263
  66.4 0.7 %pad_maximum_fusion = bf16[1024,128]{1,0:T(8,128)(2,1)} fusion(bf16[512,128]{1,0:T(8,128)(2,1)S(1)} %get-tuple-element.22, bf16[512,128]{1,0:T(8,128)(2,1)S(1)} %get-tuple-element.21), kind=kLoop, calls=%fused_computation.1 | loop fusion | flops 524288 | bytes 524288 | tf_op jit(solution)/shard_map/concatenate | solution.py:327
  (23 shorter events, 0.1 us)
Async XLA Ops:
  0.0 7.1 %copy-start = (bf16[1024,128]{1,0:T(8,128)(2,1)S(1)}, bf16[1024,128]{1,0:T(8,128)(2,1)}, u32[]{:S(2)}) copy-start(bf16[1024,128]{1,0:T(8,128)(2,1)} %refs_0_.1) | copy-start | bytes 786436
  0.0 20.4 %copy-start.2 = (bf16[512,256]{1,0:T(8,128)(2,1)S(1)}, bf16[512,256]{1,0:T(8,128)(2,1)}, u32[]{:S(2)}) copy-start(bf16[512,256]{1,0:T(8,128)(2,1)} %param.18) | copy-start | bytes 786436
  2.1 7.8 %collective-permute-start.3 = (bf16[256,128]{1,0:T(8,128)(2,1)}, bf16[256,128]{1,0:T(8,128)(2,1)S(1)}, u32[]{:S(2)}, u32[]{:S(2)}) collective-permute-start(bf16[256,128]{1,0:T(8,128)(2,1)} %get-tuple-element.13), channel_id=1, source_target_pairs={{0,4},{4,8},{8,12},{1,5},{5,9},{9,13},{2,6},{6,10},{10,14},{3,7},{... | collective-permute-start | bytes 196616 | tf_op jit(solution)/shard_map/ppermute | solution.py:296
  7.1 8.8 %collective-permute-start.1 = (bf16[1024,128]{1,0:T(8,128)(2,1)S(1)}, bf16[1024,128]{1,0:T(8,128)(2,1)S(1)}, u32[]{:S(2)}, u32[]{:S(2)}) collective-permute-start(bf16[1024,128]{1,0:T(8,128)(2,1)S(1)} %copy-done), channel_id=1, source_target_pairs={{0,2},{2,0},{1,3},{3,1},{4,6},{6,4},{5,7},{7,5},{8,10},{10,8},{9,1... | collective-permute-start | bytes 786440 | tf_op jit(solution)/shard_map/ppermute | solution.py:263
  8.7 13.9 %collective-permute-start = (bf16[1024,128]{1,0:T(8,128)(2,1)S(1)}, bf16[1024,128]{1,0:T(8,128)(2,1)S(1)}, u32[]{:S(2)}, u32[]{:S(2)}) collective-permute-start(bf16[1024,128]{1,0:T(8,128)(2,1)S(1)} %copy-done), channel_id=1, source_target_pairs={{0,1},{1,0},{2,3},{3,2},{4,5},{5,4},{6,7},{7,6},{8,9},{9,8},{10,11... | collective-permute-start | bytes 786440 | tf_op jit(solution)/shard_map/ppermute | solution.py:263
  8.7 6.6 %collective-permute-start.4 = (bf16[256,128]{1,0:T(8,128)(2,1)}, bf16[256,128]{1,0:T(8,128)(2,1)S(1)}, u32[]{:S(2)}, u32[]{:S(2)}) collective-permute-start(bf16[256,128]{1,0:T(8,128)(2,1)} %get-tuple-element.14), channel_id=1, source_target_pairs={{4,0},{8,4},{12,8},{5,1},{9,5},{13,9},{6,2},{10,6},{14,10},{7,3},{... | collective-permute-start | bytes 196616 | tf_op jit(solution)/shard_map/ppermute | solution.py:297
  15.3 6.0 %copy-start.1 = (bf16[512,128]{1,0:T(8,128)(2,1)}, bf16[512,128]{1,0:T(8,128)(2,1)S(1)}, u32[]{:S(2)}) copy-start(bf16[512,128]{1,0:T(8,128)(2,1)S(1)} %constant_dynamic-update-slice_fusion.refs_4_) | copy-start | bytes 393220
  15.3 5.1 %collective-permute-start.6 = (bf16[512,128]{1,0:T(8,128)(2,1)S(1)}, bf16[512,128]{1,0:T(8,128)(2,1)S(1)}, u32[]{:S(2)}, u32[]{:S(2)}) collective-permute-start(bf16[512,128]{1,0:T(8,128)(2,1)S(1)} %constant_dynamic-update-slice_fusion.refs_4_), channel_id=1, source_target_pairs={{0,2},{2,0},{1,3},{3,1},{4,6},{6,4},{5,7},{7,5},{8,10},{10,8},{9,1... | collective-permute-start | bytes 393224 | tf_op jit(solution)/shard_map/ppermute | solution.py:263
  15.9 5.4 %copy-start.3 = (bf16[1024,128]{1,0:T(8,128)(2,1)}, bf16[1024,128]{1,0:T(8,128)(2,1)S(1)}, u32[]{:S(2)}) copy-start(bf16[1024,128]{1,0:T(8,128)(2,1)S(1)} %collective-permute-done.1.refs_2_) | copy-start | bytes 786436
  15.9 6.7 %collective-permute-start.2 = (bf16[1024,128]{1,0:T(8,128)(2,1)S(1)}, bf16[1024,128]{1,0:T(8,128)(2,1)S(1)}, u32[]{:S(2)}, u32[]{:S(2)}) collective-permute-start(bf16[1024,128]{1,0:T(8,128)(2,1)S(1)} %collective-permute-done.1.refs_2_), channel_id=1, source_target_pairs={{0,1},{1,0},{2,3},{3,2},{4,5},{5,4},{6,7},{7,6},{8,9},{9,8},{10,11... | collective-permute-start | bytes 786440 | tf_op jit(solution)/shard_map/ppermute | solution.py:263
  15.9 6.7 %collective-permute-start.5 = (bf16[512,128]{1,0:T(8,128)(2,1)S(1)}, bf16[512,128]{1,0:T(8,128)(2,1)S(1)}, u32[]{:S(2)}, u32[]{:S(2)}) collective-permute-start(bf16[512,128]{1,0:T(8,128)(2,1)S(1)} %constant_dynamic-update-slice_fusion.refs_4_), channel_id=1, source_target_pairs={{0,1},{1,0},{2,3},{3,2},{4,5},{5,4},{6,7},{7,6},{8,9},{9,8},{10,11... | collective-permute-start | bytes 393224 | tf_op jit(solution)/shard_map/ppermute | solution.py:263
  20.4 0.9 %copy-start.7 = (bf16[512,128]{1,0:T(8,128)(2,1)}, bf16[512,128]{1,0:T(8,128)(2,1)S(1)}, u32[]{:S(2)}) copy-start(bf16[512,128]{1,0:T(8,128)(2,1)S(1)} %collective-permute-done.6.refs_6_) | copy-start | bytes 393220
  20.4 2.2 %collective-permute-start.7 = (bf16[512,128]{1,0:T(8,128)(2,1)S(1)}, bf16[512,128]{1,0:T(8,128)(2,1)S(1)}, u32[]{:S(2)}, u32[]{:S(2)}) collective-permute-start(bf16[512,128]{1,0:T(8,128)(2,1)S(1)} %collective-permute-done.6.refs_6_), channel_id=1, source_target_pairs={{0,1},{1,0},{2,3},{3,2},{4,5},{5,4},{6,7},{7,6},{8,9},{9,8},{10,11... | collective-permute-start | bytes 393224 | tf_op jit(solution)/shard_map/ppermute | solution.py:263
  22.6 0.6 copy-start.8
  22.6 0.7 %copy-start.4 = (bf16[1024,128]{1,0:T(8,128)(2,1)}, bf16[1024,128]{1,0:T(8,128)(2,1)S(1)}, u32[]{:S(2)}) copy-start(bf16[1024,128]{1,0:T(8,128)(2,1)S(1)} %collective-permute-done.refs_1_) | copy-start | bytes 786436
  22.6 0.7 %copy-start.9 = (bf16[512,128]{1,0:T(8,128)(2,1)}, bf16[512,128]{1,0:T(8,128)(2,1)S(1)}, u32[]{:S(2)}) copy-start(bf16[512,128]{1,0:T(8,128)(2,1)S(1)} %collective-permute-done.7.refs_7_) | copy-start | bytes 393220
  22.6 0.8 %copy-start.5 = (bf16[1024,128]{1,0:T(8,128)(2,1)}, bf16[1024,128]{1,0:T(8,128)(2,1)S(1)}, u32[]{:S(2)}) copy-start(bf16[1024,128]{1,0:T(8,128)(2,1)S(1)} %collective-permute-done.2.refs_3_) | copy-start | bytes 786436
  40.7 8.9 %collective-permute-start.8 = (bf16[512,256]{1,0:T(8,128)(2,1)}, bf16[512,256]{1,0:T(8,128)(2,1)S(1)}, u32[]{:S(2)}, u32[]{:S(2)}) collective-permute-start(bf16[512,256]{1,0:T(8,128)(2,1)} %attend.1.refs_0_), channel_id=1, source_target_pairs={{0,2},{2,0},{1,3},{3,1},{4,6},{6,4},{5,7},{7,5},{8,10},{10,8},{9,1... | collective-permute-start | bytes 786440 | tf_op jit(solution)/shard_map/ppermute | solution.py:263
  49.6 0.7 %copy-start.6 = (bf16[512,256]{1,0:T(8,128)(2,1)}, bf16[512,256]{1,0:T(8,128)(2,1)S(1)}, u32[]{:S(2)}) copy-start(bf16[512,256]{1,0:T(8,128)(2,1)S(1)} %collective-permute-done.8.refs_1_) | copy-start | bytes 786436
  55.7 8.1 %collective-permute-start.9 = (bf16[512,256]{1,0:T(8,128)(2,1)}, bf16[512,256]{1,0:T(8,128)(2,1)S(1)}, u32[]{:S(2)}, u32[]{:S(2)}) collective-permute-start(bf16[512,256]{1,0:T(8,128)(2,1)} %get-tuple-element.20), channel_id=1, source_target_pairs={{0,2},{2,0},{1,3},{3,1},{4,6},{6,4},{5,7},{7,5},{8,10},{10,8},{9,1... | collective-permute-start | bytes 786440 | tf_op jit(solution)/shard_map/ppermute | solution.py:263
  64.9 1.4 %collective-permute-start.10 = (bf16[512,128]{1,0:T(8,128)(2,1)S(1)}, bf16[512,128]{1,0:T(8,128)(2,1)S(1)}, u32[]{:S(2)}, u32[]{:S(2)}) collective-permute-start(bf16[512,128]{1,0:T(8,128)(2,1)S(1)} %broadcast_select_fusion.2), channel_id=1, source_target_pairs={{0,1},{1,0},{2,3},{3,2},{4,5},{5,4},{6,7},{7,6},{8,9},{9,8},{10,11... | collective-permute-start | bytes 393224 | tf_op jit(solution)/shard_map/ppermute | solution.py:263

commit v2 on v1

v2 whole, which is shorter than its diff:
```python
import functools
import math

import jax
import jax.numpy as jnp
from jax import lax
from jax.experimental import pallas as pl
from jax.experimental.pallas import tpu as pltpu
from jax.sharding import PartitionSpec as P


HD = 64


NORM_EPS = 1e-05
F32 = jnp.float32
BF16 = jnp.bfloat16
NT = (((1,), (1,)), ((), ()))
NN = (((1,), (0,)), ((), ()))


def dot(a, b, dims=NN):
    return lax.dot_general(a, b, dims, preferred_element_type=F32)


def normalize_rows(source, gain_row, shift_row):
    row_mean = jnp.mean(source, axis=-1, keepdims=True)
    spread = jnp.mean(source * source, axis=-1, keepdims=True) - row_mean * row_mean
    return (source - row_mean) * lax.rsqrt(spread + NORM_EPS) * gain_row + shift_row


def pick_body(list_ref, x_ref, up_ref, down_ref):
    rows = x_ref.shape[0]
    width = list_ref.shape[-1]
    source = x_ref[...]
    node = lax.broadcasted_iota(jnp.int32, (rows, width), 0)
    for at, out in ((1, up_ref), (0, down_ref)):
        hot = (node == list_ref[at : at + 1, :]).astype(F32).astype(BF16)
        out[...] = lax.dot_general(
            hot, source, (((0,), (0,)), ((), ())), preferred_element_type=F32
        ).astype(BF16)


def pick_rows(send_list, source):
    shape = jax.ShapeDtypeStruct((send_list.shape[1], source.shape[1]), source.dtype)
    return pl.pallas_call(pick_body, out_shape=(shape, shape), name="pick_rows")(send_list, source)


def vmem_limit(*shapes):
    total = 8 * 2**20
    for shape in shapes:
        rows, lanes = math.prod(shape.shape[:-1]), -(-shape.shape[-1] // 128) * 128
        total += -(-rows // 16) * 16 * lanes * jnp.dtype(shape.dtype).itemsize
    return min(total, 60 * 2**20)


def gather_pieces(chan_at, sub_at, pieces, xs_ref):
    cols = pieces[0].shape[1]
    for i, piece in enumerate(pieces):
        if len(pieces) == 1:
            place = slice(None)
        else:
            chan_of = chan_at if i < 2 else 1 - chan_at
            sub_of = sub_at if i % 2 == 0 else 1 - sub_at
            place = pl.ds(pl.multiple_of((chan_of * 2 + sub_of) * cols, cols), cols)
        xs_ref[:, place] = piece[...]


def project_body(chunk, count, chan_ref, sub_ref, *refs):
    pieces = refs[:count]
    gain_ref, shift_ref, wqt_ref, wk_ref, wvt_ref = refs[count : count + 5]
    qt_ref, k_ref, vt_ref, own_ref, xs_ref, ns_ref = refs[count + 5 :]
    sub_at = sub_ref[0]
    gather_pieces(chan_ref[0], sub_at, pieces, xs_ref)
    gain, shift = gain_ref[0:1, :], shift_ref[0:1, :]

    def step(j, carry):
        at = pl.ds(pl.multiple_of(j * chunk, chunk), chunk)
        normed = normalize_rows(xs_ref[at, :].astype(F32), gain, shift).astype(BF16)
        ns_ref[at, :] = normed
        k_ref[at, :] = dot(normed, wk_ref[...]).astype(BF16)
        vt_ref[:, at] = dot(wvt_ref[...], normed, NT).astype(BF16)
        return carry

    lax.fori_loop(0, xs_ref.shape[0] // chunk, step, 0, unroll=True)
    here = own_ref.shape[0]
    own = pl.ds(pl.multiple_of(sub_at * here, here), here)
    own_ref[...] = xs_ref[own, :]
    scale = 1.0 / math.sqrt(HD)
    qt = dot(wqt_ref[...], ns_ref[own, :], NT).astype(BF16)
    qt_ref[...] = (qt.astype(F32) * scale).astype(BF16)


def project(place, mains, gains, shifts, wqt, wk, wvt, here):
    rows = mains[0].shape[0]
    width = gains.shape[1]
    head_cols = wk.shape[1]
    vmem = pl.BlockSpec(memory_space=pltpu.VMEM)
    smem = pl.BlockSpec(memory_space=pltpu.SMEM)
    wide = jax.ShapeDtypeStruct((rows, width), BF16)
    outs = (
        jax.ShapeDtypeStruct((head_cols, here), BF16),
        jax.ShapeDtypeStruct((rows, head_cols), BF16),
        jax.ShapeDtypeStruct((head_cols, rows), BF16),
        jax.ShapeDtypeStruct((here, width), BF16),
    )
    return pl.pallas_call(
        functools.partial(project_body, math.gcd(rows, 256), len(mains)),
        out_shape=outs,
        in_specs=[smem] * 2 + [vmem] * (len(mains) + 5),
        out_specs=(vmem,) * 4,
        scratch_shapes=[pltpu.VMEM((rows, width), BF16)] * 2,
        compiler_params=pltpu.CompilerParams(
            vmem_limit_bytes=vmem_limit(wide, wide, *mains, *outs, wqt, wk, wvt)
        ),
        name="project",
    )(*place, *mains, gains, shifts, wqt, wk, wvt)


def extend_body(count, chan_ref, sub_ref, *refs):
    pieces = refs[:count]
    gain_ref, shift_ref, wk_ref, wvt_ref, k_ref, vt_ref = refs[count : count + 6]
    ke_ref, vte_ref, xs_ref = refs[count + 6 :]
    rows = k_ref.shape[0]
    gather_pieces(chan_ref[0], sub_ref[0], pieces, xs_ref)
    ke_ref[:rows, :] = k_ref[...]
    vte_ref[:, :rows] = vt_ref[...]
    gain, shift = gain_ref[0:1, :], shift_ref[0:1, :]
    normed = normalize_rows(xs_ref[...].astype(F32), gain, shift).astype(BF16)
    ke_ref[rows:, :] = dot(normed, wk_ref[...]).astype(BF16)
    vte_ref[:, rows:] = dot(wvt_ref[...], normed, NT).astype(BF16)


def extend(place, halos, gains, shifts, wk, wvt, keys, values_t):
    rows, head_cols = keys.shape
    extra = halos[0].shape[0]
    vmem = pl.BlockSpec(memory_space=pltpu.VMEM)
    smem = pl.BlockSpec(memory_space=pltpu.SMEM)
    outs = (
        jax.ShapeDtypeStruct((rows + extra, head_cols), BF16),
        jax.ShapeDtypeStruct((head_cols, rows + extra), BF16),
    )
    wide = jax.ShapeDtypeStruct((extra, gains.shape[1]), BF16)
    return pl.pallas_call(
        functools.partial(extend_body, len(halos)),
        out_shape=outs,
        in_specs=[smem] * 2 + [vmem] * (len(halos) + 6),
        out_specs=(vmem, vmem),
        scratch_shapes=[pltpu.VMEM(wide.shape, BF16)],
        compiler_params=pltpu.CompilerParams(
            vmem_limit_bytes=vmem_limit(wide, *halos, *outs, keys, values_t, wk, wvt)
        ),
        name="extend",
    )(*place, *halos, gains, shifts, wk, wvt, keys, values_t)


def attend_body(
    first, per_sub, blocks_own, sub_ref, live_ref, id_ref, qt_ref, bit_ref, k_ref, vt_ref,
    out_ref, s_ref,
):
    slot_count, word_count, tile = bit_ref.shape[1:]
    head_cols = qt_ref.shape[0]
    heads = head_cols // HD
    block = sub_ref[0] * per_sub + first + pl.program_id(0)
    live = live_ref[0]
    qt = qt_ref[...]
    row = lax.broadcasted_iota(jnp.int32, (head_cols, tile), 0)
    spread = jnp.concatenate(
        [jnp.where(row // HD == h, qt, jnp.zeros_like(qt)) for h in range(heads)], axis=1
    )
    key_at = lax.broadcasted_iota(jnp.int32, (tile, tile), 0)
    query_at = lax.broadcasted_iota(jnp.int32, (tile, tile), 1)
    per_word = tile // word_count
    bit_at = lax.broadcasted_iota(jnp.int32, (per_word, tile), 0)
    per_dot = math.gcd(slot_count, 2)
    peaks = [None] * heads
    starts = [pl.multiple_of(id_ref[block, t] * tile, tile) for t in range(slot_count)]
    for base in range(0, slot_count, per_dot):
        block_keys = [k_ref[pl.ds(starts[base + i], tile), :] for i in range(per_dot)]
        scores = dot(jnp.concatenate(block_keys, axis=0), spread)
        for i in range(per_dot):
            t = base + i
            key_id = id_ref[block, t]
            limit = jnp.where(key_id >= blocks_own, tile, live - key_id * tile)
            usable = key_at < limit
            if t == 0:
                usable = usable | (key_at == query_at)
            words = jnp.concatenate(
                [
                    jnp.right_shift(
                        jnp.broadcast_to(bit_ref[0, t, w : w + 1, :], (per_word, tile)), bit_at
                    )
                    & 1
                    for w in range(word_count)
                ],
                axis=0,
            )
            allowed = (words == 1) & usable
            for h in range(heads):
                cols = slice(h * tile, (h + 1) * tile)
                part = jnp.where(allowed, scores[i * tile : (i + 1) * tile, cols], -jnp.inf)
                s_ref[t * tile : (t + 1) * tile, cols] = part
                top = jnp.max(part.reshape(tile // 8, 8, tile), axis=0)
                peaks[h] = top if peaks[h] is None else jnp.maximum(peaks[h], top)
    peak = jnp.max(jnp.concatenate(peaks, axis=1), axis=0, keepdims=True)
    group = math.gcd(heads, 2)
    mixed = [None] * (heads // group)
    total = None
    for t in range(0, slot_count, per_dot):
        weights = jnp.exp(s_ref[t * tile : (t + per_dot) * tile, :] - peak)
        part = jnp.sum(weights.reshape(per_dot * tile // 8, 8, heads * tile), axis=0)
        total = part if total is None else total + part
        weights = weights.astype(BF16)
        for g in range(heads // group):
            values = jnp.concatenate(
                [
                    vt_ref[g * group * HD : (g + 1) * group * HD, pl.ds(starts[t + i], tile)]
                    for i in range(per_dot)
                ],
                axis=1,
            )
            add = dot(values, weights[:, g * group * tile : (g + 1) * group * tile])
            mixed[g] = add if mixed[g] is None else mixed[g] + add
    total = jnp.sum(total, axis=0, keepdims=True)
    pieces = []
    for h in range(heads):
        g, i = divmod(h, group)
        own = mixed[g][i * HD : (i + 1) * HD, i * tile : (i + 1) * tile]
        pieces.append(own / total[:, h * tile : (h + 1) * tile])
    out_ref[...] = jnp.concatenate(pieces, axis=0).T.astype(BF16)


def attend(sub_id, live_counts, tile_keys, queries_t, tile_bits, keys, values_t, first, count):
    blocks_own, slot_count, word_count, tile = tile_bits.shape
    head_cols, here = queries_t.shape
    total = keys.shape[0]
    per_sub = here // tile
    heads = head_cols // HD
    scratch = jax.ShapeDtypeStruct((slot_count * tile, heads * tile), F32)
    return pl.pallas_call(
        functools.partial(attend_body, first, per_sub, blocks_own),
        out_shape=jax.ShapeDtypeStruct((count * tile, head_cols), BF16),
        grid_spec=pltpu.PrefetchScalarGridSpec(
            num_scalar_prefetch=3,
            grid=(count,),
            in_specs=[
                pl.BlockSpec((head_cols, tile), lambda i, m, n, k: (0, first + i)),
                pl.BlockSpec(
                    (1, slot_count, word_count, tile),
                    lambda i, m, n, k: (m[0] * per_sub + first + i, 0, 0, 0),
                ),
                pl.BlockSpec((total, head_cols), lambda i, m, n, k: (0, 0)),
                pl.BlockSpec((head_cols, total), lambda i, m, n, k: (0, 0)),
            ],
            out_specs=pl.BlockSpec((tile, head_cols), lambda i, m, n, k: (i, 0)),
            scratch_shapes=[pltpu.VMEM(scratch.shape, F32)],
        ),
        compiler_params=pltpu.CompilerParams(
            vmem_limit_bytes=vmem_limit(scratch, scratch, keys, keys, values_t, values_t)
        ),
        name="attend",
    )(sub_id, live_counts, tile_keys, queries_t, tile_bits, keys, values_t)


def feed_body(first_row, chunk, paired, chan_ref, *refs):
    count = 2 if paired else 1
    mixed = refs[:count]
    x_ref, wo_ref, gain_ref, shift_ref, in_ref, out_w_ref, send_ref, keep_ref = refs[count:]
    chan_at = chan_ref[0]
    width = x_ref.shape[1]
    here = mixed[0].shape[0]
    gain, shift = gain_ref[1:2, :], shift_ref[1:2, :]

    def step(j, carry):
        at = pl.ds(pl.multiple_of(j * chunk, chunk), chunk)
        after = x_ref[pl.ds(pl.multiple_of(first_row + j * chunk, chunk), chunk), :].astype(F32)
        for i in range(count):
            cols = mixed[i].shape[1]
            if paired:
                chan_of = chan_at if i == 0 else 1 - chan_at
                weight = wo_ref[pl.ds(pl.multiple_of(chan_of * cols, cols), cols), :]
            else:
                weight = wo_ref[...]
            after = after + dot(mixed[i][at, :], weight)
        normed = normalize_rows(after, gain, shift).astype(BF16)
        hidden = jax.nn.gelu(dot(normed, in_ref[...], NT)).astype(BF16)
        update = dot(hidden, out_w_ref[...])
        if paired:
            half = width // 2
            first = chan_at == 0
            send_ref[at, :] = jnp.where(first, update[:, half:], update[:, :half]).astype(BF16)
            both = after + update
            keep_ref[at, :] = jnp.where(first, both[:, :half], both[:, half:])
        else:
            send_ref[at, :] = update.astype(BF16)
            keep_ref[at, :] = after
        return carry

    lax.fori_loop(0, here // chunk, step, 0)


def feed(chan_id, mixed, own_x, out_weight, gains, shifts, ffn_in, ffn_out, first_row):
    paired = len(mixed) == 2
    here, width = mixed[0].shape[0], own_x.shape[1]
    cols = width // 2 if paired else width
    vmem = pl.BlockSpec(memory_space=pltpu.VMEM)
    smem = pl.BlockSpec(memory_space=pltpu.SMEM)
    outs = (jax.ShapeDtypeStruct((here, cols), BF16), jax.ShapeDtypeStruct((here, cols), F32))
    return pl.pallas_call(
        functools.partial(feed_body, first_row, math.gcd(here, 256), paired),
        out_shape=outs,
        in_specs=[smem] + [vmem] * (len(mixed) + 6),
        out_specs=(vmem, vmem),
        compiler_params=pltpu.CompilerParams(
            vmem_limit_bytes=vmem_limit(*mixed, *outs, own_x, out_weight, ffn_in, ffn_out)
        ),
        name="feed",
    )(chan_id, *mixed, own_x, out_weight, gains, shifts, ffn_in, ffn_out)


def swap(array, axis):
    return lax.ppermute(array, axis, [(0, 1), (1, 0)])


def on_device(
    node_state,
    norm_gains,
    norm_shifts,
    query_weight,
    key_weight,
    value_weight,
    out_weight,
    ffn_in,
    ffn_out,
    live_counts,
    send_rows,
    tile_keys,
    tile_bits,
):
    n_chan = lax.axis_size("chan")
    n_sub = lax.axis_size("sub")
    n_space = lax.axis_size("space")
    paired = n_chan == 2 and n_sub == 2
    chan_at = lax.axis_index("chan")
    sub_at = lax.axis_index("sub")
    node_count, local_cols = node_state.shape
    tile = tile_bits.shape[-1]
    here = node_count // n_sub
    place = (chan_at.astype(jnp.int32).reshape(1), sub_at.astype(jnp.int32).reshape(1))
    up = [(i, i + 1) for i in range(n_space - 1)]
    down = [(i + 1, i) for i in range(n_space - 1)]

    if paired:
        across = swap(node_state, "chan")
        mains = [node_state, swap(node_state, "sub"), across, swap(across, "sub")]
    else:
        mains = [lax.all_gather(node_state, ("chan", "sub"), axis=1, tiled=True)]
    upward, downward = pick_rows(send_rows[0], node_state)
    lower = lax.ppermute(upward, "space", up)
    upper = lax.ppermute(downward, "space", down)
    halo = jnp.concatenate([lower, upper], axis=0)
    if paired:
        halo_across = swap(halo, "chan")
        halos = [halo, swap(halo, "sub"), halo_across, swap(halo_across, "sub")]
    else:
        halos = [lax.all_gather(halo, ("chan", "sub"), axis=1, tiled=True)]
    values_w = value_weight.T
    queries_t, keys, values_t, own_x = project(
        place, mains, norm_gains, norm_shifts, query_weight.T, key_weight, values_w, here
    )
    keys, values_t = extend(
        place, halos, norm_gains, norm_shifts, key_weight, values_w, keys, values_t
    )
    blocks_here = here // tile
    parts = math.gcd(blocks_here, 2)
    count = blocks_here // parts
    attended = []
    for i in range(parts):
        attended.append(
            attend(
                place[1], live_counts, tile_keys, queries_t, tile_bits, keys, values_t,
                i * count, count,
            )
        )
    finals = []
    for i in range(parts):
        if paired:
            mixed = [attended[i], swap(attended[i], "chan")]
        else:
            mixed = [lax.all_gather(attended[i], "chan", axis=1, tiled=True)]
        first_row = i * count * tile
        send, keep = feed(
            place[0], mixed, own_x, out_weight, norm_gains, norm_shifts, ffn_in, ffn_out,
            first_row,
        )
        if paired:
            total = keep + swap(send, "chan").astype(F32)
        else:
            width = keep.shape[1] // n_chan
            kept = lax.dynamic_slice_in_dim(keep, chan_at * width, width, 1)
            added = lax.psum_scatter(send, "chan", scatter_dimension=1, tiled=True)
            total = kept + added.astype(F32)
        position = sub_at * here + first_row + jnp.arange(total.shape[0], dtype=jnp.int32)
        finals.append(jnp.where((position < live_counts[0])[:, None], total, 0.0).astype(BF16))
    if paired:
        first = sub_at == 0
        mine, theirs = [], []
        for result in finals:
            left, right = result[:, :local_cols], result[:, local_cols:]
            mine.append(jnp.where(first, left, right))
            theirs.append(swap(jnp.where(first, right, left), "sub"))
        low = [jnp.where(first, a, b) for a, b in zip(mine, theirs)]
        high = [jnp.where(first, b, a) for a, b in zip(mine, theirs)]
        return jnp.concatenate(low + high, axis=0)
    result = jnp.concatenate(finals, axis=0)
    return lax.all_to_all(result, "sub", split_axis=1, concat_axis=0, tiled=True)


def solution(mesh):
    in_specs = (
        P(("ens", "space"), ("chan", "sub")),
        P(),
        P(),
        P(None, "chan"),
        P(None, "chan"),
        P(None, "chan"),
        P(),
        P("chan", None),
        P("chan", None),
        P("space"),
        P("space", None, None),
        P("space", None),
        P("space", None, None, None),
    )
    out_specs = P(("ens", "space"), ("chan", "sub"))

    return jax.shard_map(
        on_device, mesh=mesh, in_specs=in_specs, out_specs=out_specs, check_vma=False
    )
```

time: 67.4 us -> 54.1 us (0.80)
  waiting for transfers between devices: 26.6 us -> 14 us
  Pallas kernels: 24.7 us -> 17.4 us
  local copies, waits for them, and re-layouts: 2.43 us -> 6.58 us
  starting transfers between devices: 10 us -> 12.8 us
  other arithmetic: 2.6 us -> 1.9 us
    ppermute x9 -> x12, waiting for transfers between devices: 21.3 us -> 8.77 us  [swap(): return lax.ppermute(array, axis, [(0, 1), (1, 0)])]
    pallas_call x3 -> x6, Pallas kernels: 22.5 us -> 15.2 us  [the longest x2 7.99 us: attend(): pl.pallas_call(functools.partial(attend_body, first, per_sub, blocks_own)...]
    ppermute x9 -> x12, starting transfers between devices: 3.82 us -> 8.04 us  [swap(): return lax.ppermute(array, axis, [(0, 1), (1, 0)])]
    unnamed x22 -> x39, local copies, waits for them, and re-layouts: 2.42 us -> 6.57 us
    ppermute x1, starting transfers between devices: 4.95 us -> 3.47 us  [on_device(): lower = lax.ppermute(upward, 'space', up)]
    ppermute x1, waiting for transfers between devices: 5.28 us -> 4.38 us  [on_device(): upper = lax.ppermute(downward, 'space', down)]
    ppermute x1, waiting for transfers between devices: 0.01 us -> 0.81 us  [on_device(): lower = lax.ppermute(upward, 'space', up)]
  transfers between devices with their start and end apart: 11 -> 14, of which waited for: 5 -> 6; matrix products, arithmetic and copies ran while one was open for 2% -> 3% of each run, Pallas kernels for 0% -> 23%
where the time goes in v2:
time: 54.1 us; the launch traced here: 53.6 us
  Pallas kernels  17.4 us (32%)
  waiting for transfers between devices  14 us (26%)
  starting transfers between devices  12.8 us (24%)
  local copies, waits for them, and re-layouts  6.58 us (12%)
  other arithmetic  1.9 us (4%)
  between operations  0.96 us (2%)
    ppermute x12, waiting for transfers between devices, swap(): return lax.ppermute(array, axis, [(0, 1), (1, 0)])  8.77 us
    ppermute x12, starting transfers between devices, swap(): return lax.ppermute(array, axis, [(0, 1), (1, 0)])  8.04 us
    pallas_call x2, Pallas kernels, attend(): pl.pallas_call(functools.partial(attend_body, first, per_sub, blocks_own)...  7.99 us
    unnamed x39, local copies, waits for them, and re-layouts  6.57 us
    pallas_call x2, Pallas kernels, feed(): pl.pallas_call(functools.partial(feed_body, first_row, math.gcd(here, 256...  4.91 us
    ppermute x1, waiting for transfers between devices, on_device(): upper = lax.ppermute(downward, 'space', down)  4.38 us
    ppermute x1, starting transfers between devices, on_device(): lower = lax.ppermute(upward, 'space', up)  3.47 us
    pallas_call x1, Pallas kernels, pick_rows(): pl.pallas_call(pick_body, out_shape=(shape, shape), name='pick_rows')  2.13 us
  transfers between devices with their start and end apart: 14, of which 6 were waited for; matrix products, arithmetic and copies ran while one was open for 3% of the time, Pallas kernels for 23%

profile of v2, /device:TPU:0, one launch (start us, length us, event | category | flops | bytes accessed | tf_op | source)
XLA Modules:
  0.0 53.6 jit_solution(7247689703830005401)
XLA Ops:
  0.0 3.0 %collective-permute-start.1 = (bf16[1024,128]{1,0:T(8,128)(2,1)}, bf16[1024,128]{1,0:T(8,128)(2,1)S(1)}, u32[]{:S(2)}, u32[]{:S(2)}) collective-permute-start(bf16[1024,128]{1,0:T(8,128)(2,1)} %x_ref.1), channel_id=1, source_target_pairs={{0,2},{2,0},{1,3},{3,1},{4,6},{6,4},{5,7},{7,5},{8,10},{10,8},{9,1... | collective-permute-start | bytes 786440 | tf_op jit(solution)/shard_map/ppermute | solution.py:322
  3.0 2.1 %pick_rows.1 = (bf16[256,128]{1,0:T(8,128)(2,1)}, bf16[256,128]{1,0:T(8,128)(2,1)}) custom-call(s32[2,256]{1,0:T(2,128)} %bitcast.11, bf16[1024,128]{1,0:T(8,128)(2,1)} %x_ref.1), custom_call_target="tpu_custom_call" | custom-call | tf_op jit(solution)/shard_map/pick_rows/pallas_call | solution.py:46
  5.1 3.5 %collective-permute-start.3 = (bf16[256,128]{1,0:T(8,128)(2,1)}, bf16[256,128]{1,0:T(8,128)(2,1)S(1)}, u32[]{:S(2)}, u32[]{:S(2)}) collective-permute-start(bf16[256,128]{1,0:T(8,128)(2,1)} %get-tuple-element.18), channel_id=1, source_target_pairs={{0,4},{4,8},{8,12},{1,5},{5,9},{9,13},{2,6},{6,10},{10,14},{3,7},{... | collective-permute-start | bytes 196616 | tf_op jit(solution)/shard_map/ppermute | solution.py:359
  8.7 1.3 %collective-permute-start.4 = (bf16[256,128]{1,0:T(8,128)(2,1)}, bf16[256,128]{1,0:T(8,128)(2,1)S(1)}, u32[]{:S(2)}, u32[]{:S(2)}) collective-permute-start(bf16[256,128]{1,0:T(8,128)(2,1)} %get-tuple-element.19), channel_id=1, source_target_pairs={{4,0},{8,4},{12,8},{5,1},{9,5},{13,9},{6,2},{10,6},{14,10},{7,3},{... | collective-permute-start | bytes 196616 | tf_op jit(solution)/shard_map/ppermute | solution.py:360
  10.0 0.8 %collective-permute-done.3 = bf16[256,128]{1,0:T(8,128)(2,1)S(1)} collective-permute-done((bf16[256,128]{1,0:T(8,128)(2,1)}, bf16[256,128]{1,0:T(8,128)(2,1)S(1)}, u32[]{:S(2)}, u32[]{:S(2)}) %collective-permute-start.3) | collective-permute-done | bytes 65568 | tf_op jit(solution)/shard_map/ppermute | solution.py:359
  10.9 4.4 %collective-permute-done.4 = bf16[256,128]{1,0:T(8,128)(2,1)S(1)} collective-permute-done((bf16[256,128]{1,0:T(8,128)(2,1)}, bf16[256,128]{1,0:T(8,128)(2,1)S(1)}, u32[]{:S(2)}, u32[]{:S(2)}) %collective-permute-start.4) | collective-permute-done | bytes 65568 | tf_op jit(solution)/shard_map/ppermute | solution.py:360
  15.3 0.6 %collective-permute-start.6 = (bf16[512,128]{1,0:T(8,128)(2,1)S(1)}, bf16[512,128]{1,0:T(8,128)(2,1)S(1)}, u32[]{:S(2)}, u32[]{:S(2)}) collective-permute-start(bf16[512,128]{1,0:T(8,128)(2,1)S(1)} %constant_dynamic-update-slice_fusion.refs_0_), channel_id=1, source_target_pairs={{0,2},{2,0},{1,3},{3,1},{4,6},{6,4},{5,7},{7,5},{8,10},{10,8},{9,1... | collective-permute-start | bytes 393224 | tf_op jit(solution)/shard_map/ppermute | solution.py:322
  15.9 4.5 %collective-permute-done.6.refs_2_ = bf16[512,128]{1,0:T(8,128)(2,1)S(1)} collective-permute-done((bf16[512,128]{1,0:T(8,128)(2,1)S(1)}, bf16[512,128]{1,0:T(8,128)(2,1)S(1)}, u32[]{:S(2)}, u32[]{:S(2)}) %collective-permute-start.6) | collective-permute-done | bytes 131104 | tf_op jit(solution)/shard_map/ppermute | solution.py:322
  20.4 0.1 copy.15
  20.5 0.8 %copy-done.17 = bf16[512,256]{1,0:T(8,128)(2,1)S(1)} copy-done((bf16[512,256]{1,0:T(8,128)(2,1)S(1)}, bf16[512,256]{1,0:T(8,128)(2,1)}, u32[]{:S(2)}) %copy-start.17) | copy-done | bytes 262168
  22.3 0.6 %copy-done.13 = f32[2,512]{1,0:T(2,128)S(1)} copy-done((f32[2,512]{1,0:T(2,128)S(1)}, f32[2,512]{1,0:T(2,128)}, u32[]{:S(2)}) %copy-start.13) | copy-done | bytes 4120
  22.9 1.5 %project.1 = (bf16[256,512]{1,0:T(8,128)(2,1)S(1)}, bf16[1024,256]{1,0:T(8,128)(2,1)S(1)}, bf16[256,1024]{1,0:T(8,128)(2,1)S(1)}, bf16[512,512]{1,0:T(8,128)(2,1)S(1)}) custom-call(s32[1]{0:T(128)} %bitcast.1.chan_ref, s32[1]{0:T(128)} %bitcast.2.sub_ref, bf16[1024,128]{1,0:T(8,128)(2,1)S(1)} %copy-done.7, ...), custom_call_target="tpu_custom_call" | custom-call | tf_op jit(solution)/shard_map/project/pallas_call | solution.py:107
  24.4 0.9 %extend.1 = (bf16[1536,256]{1,0:T(8,128)(2,1)S(1)}, bf16[256,1536]{1,0:T(8,128)(2,1)S(1)}) custom-call(s32[1]{0:T(128)} %bitcast.1.chan_ref, s32[1]{0:T(128)} %bitcast.2.sub_ref, bf16[512,128]{1,0:T(8,128)(2,1)S(1)} %constant_dynamic-update-slice_fusion.refs_0_, bf16[512,128]{1,0:T(8,128)(2,1)S(1)} %collective-permute-done.5.refs_1_, ...), custom_call_target="tpu_custom_call" | custom-call | tf_op jit(solution)/shard_map/extend/pallas_call | solution.py:144
  25.3 0.3 copy-done.11
  25.5 0.5 copy-done.15
  26.0 4.3 %attend.2.refs_0_ = bf16[256,256]{1,0:T(8,128)(2,1)} custom-call(s32[1]{0:T(128)} %bitcast.2.sub_ref, s32[1]{0:T(128)} %copy.17.live_ref, s32[8,12]{1,0:T(8,128)S(1)} %copy-done.15, bf16[256,512]{1,0:T(8,128)(2,1)S(1)} %get-tuple-element.17.qt_ref, s32[8,12,4,128]{3,2,1,0:T(4,128)S(1)} %copy-done.11, bf16[1536,256]{1,0:T(8,128)(2,1)S(1)} %get-tuple-element.22.k_ref, ...), custom_call_target="tpu_custom_call" | custom-call | tf_op jit(solution)/shard_map/attend/pallas_call | solution.py:240
  30.3 0.5 collective-permute-start.8
  30.9 1.1 %copy-done.3 = bf16[256,1536]{1,0:T(8,128)(2,1)S(1)} copy-done((bf16[256,1536]{1,0:T(8,128)(2,1)S(1)}, bf16[256,1536]{1,0:T(8,128)(2,1)}, u32[]{:S(2)}) %copy-start.3) | copy-done | bytes 786456
  32.0 0.9 %copy-done.10 = bf16[256,512]{1,0:T(8,128)(2,1)S(1)} copy-done((bf16[256,512]{1,0:T(8,128)(2,1)S(1)}, bf16[256,512]{1,0:T(8,128)(2,1)}, u32[]{:S(2)}) %copy-start.10) | copy-done | bytes 262168
  32.9 0.9 %copy-done.12 = s32[8,12,4,128]{3,2,1,0:T(4,128)S(1)} copy-done((s32[8,12,4,128]{3,2,1,0:T(4,128)S(1)}, s32[8,12,4,128]{3,2,1,0:T(4,128)}, u32[]{:S(2)}) %copy-start.12) | copy-done | bytes 196632
  33.9 3.7 %attend.3.refs_0_ = bf16[256,256]{1,0:T(8,128)(2,1)S(1)} custom-call(s32[1]{0:T(128)} %bitcast.2.sub_ref, s32[1]{0:T(128)} %copy.17.live_ref, s32[8,12]{1,0:T(8,128)S(1)} %copy-done.15, bf16[256,512]{1,0:T(8,128)(2,1)S(1)} %copy-done.10, s32[8,12,4,128]{3,2,1,0:T(4,128)S(1)} %copy-done.12, bf16[1536,256]{1,0:T(8,128)(2,1)S(1)} %get-tuple-element.22.k_ref, ...), custom_call_target="tpu_custom_call" | custom-call | tf_op jit(solution)/shard_map/attend/pallas_call | solution.py:240
  37.6 1.6 %collective-permute-start.11 = (bf16[256,256]{1,0:T(8,128)(2,1)S(1)}, bf16[256,256]{1,0:T(8,128)(2,1)}, u32[]{:S(2)}, u32[]{:S(2)}) collective-permute-start(bf16[256,256]{1,0:T(8,128)(2,1)S(1)} %attend.3.refs_0_), channel_id=1, source_target_pairs={{0,2},{2,0},{1,3},{3,1},{4,6},{6,4},{5,7},{7,5},{8,10},{10,8},{9,1... | collective-permute-start | bytes 393224 | tf_op jit(solution)/shard_map/ppermute | solution.py:322
  39.2 1.0 %copy-done.6 = bf16[512,512]{1,0:T(8,128)(2,1)S(1)} copy-done((bf16[512,512]{1,0:T(8,128)(2,1)S(1)}, bf16[512,512]{1,0:T(8,128)(2,1)}, u32[]{:S(2)}) %copy-start.6) | copy-done | bytes 524312
  40.2 2.8 %feed.2 = (bf16[256,256]{1,0:T(8,128)(2,1)}, f32[256,256]{1,0:T(8,128)S(1)}) custom-call(s32[1]{0:T(128)} %bitcast.1.chan_ref, bf16[256,256]{1,0:T(8,128)(2,1)} %attend.2.refs_0_, bf16[256,256]{1,0:T(8,128)(2,1)} %collective-permute-done.8.refs_1_, bf16[512,512]{1,0:T(8,128)(2,1)S(1)} %copy-done.6, bf16[512,512]{1,0:T(8,128)(2,1)S(1)} %copy-done.4, ...), custom_call_target="tpu_custom_call" | custom-call | tf_op jit(solution)/shard_map/feed/pallas_call | solution.py:309
  43.0 0.5 collective-permute-start.9
  43.6 2.1 %feed.3 = (bf16[256,256]{1,0:T(8,128)(2,1)S(1)}, f32[256,256]{1,0:T(8,128)S(1)}) custom-call(s32[1]{0:T(128)} %bitcast.1.chan_ref, bf16[256,256]{1,0:T(8,128)(2,1)S(1)} %attend.3.refs_0_, bf16[256,256]{1,0:T(8,128)(2,1)} %collective-permute-done.11.refs_1_, bf16[512,512]{1,0:T(8,128)(2,1)S(1)} %copy-done.6, bf16[512,512]{1,0:T(8,128)(2,1)S(1)} %copy-done.4, ...), custom_call_target="tpu_custom_call" | custom-call | tf_op jit(solution)/shard_map/feed/pallas_call | solution.py:309
  45.7 1.6 %collective-permute-start.12 = (bf16[256,256]{1,0:T(8,128)(2,1)S(1)}, bf16[256,256]{1,0:T(8,128)(2,1)S(1)}, u32[]{:S(2)}, u32[]{:S(2)}) collective-permute-start(bf16[256,256]{1,0:T(8,128)(2,1)S(1)} %get-tuple-element.28), channel_id=1, source_target_pairs={{0,2},{2,0},{1,3},{3,1},{4,6},{6,4},{5,7},{7,5},{8,10},{10,8},{9,1... | collective-permute-start | bytes 393224 | tf_op jit(solution)/shard_map/ppermute | solution.py:322
  47.2 2.0 %collective-permute-done.9 = bf16[256,256]{1,0:T(8,128)(2,1)} collective-permute-done((bf16[256,256]{1,0:T(8,128)(2,1)}, bf16[256,256]{1,0:T(8,128)(2,1)}, u32[]{:S(2)}, u32[]{:S(2)}) %collective-permute-start.9) | collective-permute-done | bytes 131104 | tf_op jit(solution)/shard_map/ppermute | solution.py:322
  49.3 1.0 %select_convert_fusion.1 = bf16[256,256]{1,0:T(8,128)(2,1)S(1)} fusion(f32[256,256]{1,0:T(8,128)S(1)} %get-tuple-element.25, bf16[256,256]{1,0:T(8,128)(2,1)} %collective-permute-done.9, pred[256]{0:T(512)(128)(4,1)S(1)} %add_compare_fusion.1), kind=kLoop, calls=%fused_computation.2 | loop fusion | flops 262144 | bytes 524544 | tf_op jit(solution)/shard_map/convert_element_type | solution.py:404
  50.4 1.0 %collective-permute-done.12 = bf16[256,256]{1,0:T(8,128)(2,1)S(1)} collective-permute-done((bf16[256,256]{1,0:T(8,128)(2,1)S(1)}, bf16[256,256]{1,0:T(8,128)(2,1)S(1)}, u32[]{:S(2)}, u32[]{:S(2)}) %collective-permute-start.12) | collective-permute-done | bytes 131104 | tf_op jit(solution)/shard_map/ppermute | solution.py:322
  51.6 1.2 %collective-permute-done.13 = bf16[256,128]{1,0:T(8,128)(2,1)S(1)} collective-permute-done((bf16[256,128]{1,0:T(8,128)(2,1)S(1)}, bf16[256,128]{1,0:T(8,128)(2,1)S(1)}, u32[]{:S(2)}, u32[]{:S(2)}) %collective-permute-start.13) | collective-permute-done | bytes 65568 | tf_op jit(solution)/shard_map/ppermute | solution.py:322
  52.9 0.7 %pad_maximum_fusion = bf16[1024,128]{1,0:T(8,128)(2,1)} fusion(bf16[256,128]{1,0:T(8,128)(2,1)S(1)} %get-tuple-element.32, bf16[256,128]{1,0:T(8,128)(2,1)S(1)} %get-tuple-element.30, bf16[256,128]{1,0:T(8,128)(2,1)S(1)} %get-tuple-element.31, bf16[256,128]{1,0:T(8,128)(2,1)S(1)} %get-tuple-element.29), kind=kLoop, calls=%fused_computation | loop fusion | flops 1048576 | bytes 524288 | tf_op jit(solution)/shard_map/concatenate | solution.py:414
  (52 shorter events, 0.8 us)
Async XLA Ops:
  0.0 8.6 %copy-start.7 = (bf16[1024,128]{1,0:T(8,128)(2,1)S(1)}, bf16[1024,128]{1,0:T(8,128)(2,1)}, u32[]{:S(2)}) copy-start(bf16[1024,128]{1,0:T(8,128)(2,1)} %x_ref.1) | copy-start | bytes 786436
  0.0 10.8 %collective-permute-start.1 = (bf16[1024,128]{1,0:T(8,128)(2,1)}, bf16[1024,128]{1,0:T(8,128)(2,1)S(1)}, u32[]{:S(2)}, u32[]{:S(2)}) collective-permute-start(bf16[1024,128]{1,0:T(8,128)(2,1)} %x_ref.1), channel_id=1, source_target_pairs={{0,2},{2,0},{1,3},{3,1},{4,6},{6,4},{5,7},{7,5},{8,10},{10,8},{9,1... | collective-permute-start | bytes 786440 | tf_op jit(solution)/shard_map/ppermute | solution.py:322
  3.0 17.4 %copy-start.16 = (bf16[512,256]{1,0:T(8,128)(2,1)S(1)}, bf16[512,256]{1,0:T(8,128)(2,1)}, u32[]{:S(2)}) copy-start(bf16[512,256]{1,0:T(8,128)(2,1)} %param.18) | copy-start | bytes 786436
  5.1 5.7 %collective-permute-start.3 = (bf16[256,128]{1,0:T(8,128)(2,1)}, bf16[256,128]{1,0:T(8,128)(2,1)S(1)}, u32[]{:S(2)}, u32[]{:S(2)}) collective-permute-start(bf16[256,128]{1,0:T(8,128)(2,1)} %get-tuple-element.18), channel_id=1, source_target_pairs={{0,4},{4,8},{8,12},{1,5},{5,9},{9,13},{2,6},{6,10},{10,14},{3,7},{... | collective-permute-start | bytes 196616 | tf_op jit(solution)/shard_map/ppermute | solution.py:359
  8.6 13.6 %collective-permute-start = (bf16[1024,128]{1,0:T(8,128)(2,1)S(1)}, bf16[1024,128]{1,0:T(8,128)(2,1)S(1)}, u32[]{:S(2)}, u32[]{:S(2)}) collective-permute-start(bf16[1024,128]{1,0:T(8,128)(2,1)S(1)} %copy-done.7), channel_id=1, source_target_pairs={{0,1},{1,0},{2,3},{3,2},{4,5},{5,4},{6,7},{7,6},{8,9},{9,8},{10,11... | collective-permute-start | bytes 786440 | tf_op jit(solution)/shard_map/ppermute | solution.py:322
  8.7 6.6 %collective-permute-start.4 = (bf16[256,128]{1,0:T(8,128)(2,1)}, bf16[256,128]{1,0:T(8,128)(2,1)S(1)}, u32[]{:S(2)}, u32[]{:S(2)}) collective-permute-start(bf16[256,128]{1,0:T(8,128)(2,1)} %get-tuple-element.19), channel_id=1, source_target_pairs={{4,0},{8,4},{12,8},{5,1},{9,5},{13,9},{6,2},{10,6},{14,10},{7,3},{... | collective-permute-start | bytes 196616 | tf_op jit(solution)/shard_map/ppermute | solution.py:360
  10.8 11.4 %collective-permute-start.2 = (bf16[1024,128]{1,0:T(8,128)(2,1)S(1)}, bf16[1024,128]{1,0:T(8,128)(2,1)S(1)}, u32[]{:S(2)}, u32[]{:S(2)}) collective-permute-start(bf16[1024,128]{1,0:T(8,128)(2,1)S(1)} %collective-permute-done.1.refs_2_), channel_id=1, source_target_pairs={{0,1},{1,0},{2,3},{3,2},{4,5},{5,4},{6,7},{7,6},{8,9},{9,8},{10,11... | collective-permute-start | bytes 786440 | tf_op jit(solution)/shard_map/ppermute | solution.py:322
  15.3 5.1 %collective-permute-start.6 = (bf16[512,128]{1,0:T(8,128)(2,1)S(1)}, bf16[512,128]{1,0:T(8,128)(2,1)S(1)}, u32[]{:S(2)}, u32[]{:S(2)}) collective-permute-start(bf16[512,128]{1,0:T(8,128)(2,1)S(1)} %constant_dynamic-update-slice_fusion.refs_0_), channel_id=1, source_target_pairs={{0,2},{2,0},{1,3},{3,1},{4,6},{6,4},{5,7},{7,5},{8,10},{10,8},{9,1... | collective-permute-start | bytes 393224 | tf_op jit(solution)/shard_map/ppermute | solution.py:322
  15.9 8.5 %collective-permute-start.5 = (bf16[512,128]{1,0:T(8,128)(2,1)S(1)}, bf16[512,128]{1,0:T(8,128)(2,1)S(1)}, u32[]{:S(2)}, u32[]{:S(2)}) collective-permute-start(bf16[512,128]{1,0:T(8,128)(2,1)S(1)} %constant_dynamic-update-slice_fusion.refs_0_), channel_id=1, source_target_pairs={{0,1},{1,0},{2,3},{3,2},{4,5},{5,4},{6,7},{7,6},{8,9},{9,8},{10,11... | collective-permute-start | bytes 393224 | tf_op jit(solution)/shard_map/ppermute | solution.py:322
  20.4 4.0 %collective-permute-start.7 = (bf16[512,128]{1,0:T(8,128)(2,1)S(1)}, bf16[512,128]{1,0:T(8,128)(2,1)S(1)}, u32[]{:S(2)}, u32[]{:S(2)}) collective-permute-start(bf16[512,128]{1,0:T(8,128)(2,1)S(1)} %collective-permute-done.6.refs_2_), channel_id=1, source_target_pairs={{0,1},{1,0},{2,3},{3,2},{4,5},{5,4},{6,7},{7,6},{8,9},{9,8},{10,11... | collective-permute-start | bytes 393224 | tf_op jit(solution)/shard_map/ppermute | solution.py:322
  20.4 1.0 %copy-start.17 = (bf16[512,256]{1,0:T(8,128)(2,1)S(1)}, bf16[512,256]{1,0:T(8,128)(2,1)}, u32[]{:S(2)}) copy-start(bf16[512,256]{1,0:T(8,128)(2,1)} %param.16) | copy-start | bytes 786436
  21.3 0.9 %copy-start.8 = (bf16[512,256]{1,0:T(8,128)(2,1)S(1)}, bf16[512,256]{1,0:T(8,128)(2,1)}, u32[]{:S(2)}) copy-start(bf16[512,256]{1,0:T(8,128)(2,1)} %refs_6_.3) | copy-start | bytes 786436
  21.5 0.8 %copy-start.14 = (f32[2,512]{1,0:T(2,128)S(1)}, f32[2,512]{1,0:T(2,128)}, u32[]{:S(2)}) copy-start(f32[2,512]{1,0:T(2,128)} %refs_5_.7) | copy-start | bytes 12292
  22.1 0.7 %copy-start.13 = (f32[2,512]{1,0:T(2,128)S(1)}, f32[2,512]{1,0:T(2,128)}, u32[]{:S(2)}) copy-start(f32[2,512]{1,0:T(2,128)} %refs_4_.7) | copy-start | bytes 12292
  24.3 0.9 %copy-start.5 = (bf16[512,512]{1,0:T(8,128)(2,1)}, bf16[512,512]{1,0:T(8,128)(2,1)S(1)}, u32[]{:S(2)}) copy-start(bf16[512,512]{1,0:T(8,128)(2,1)S(1)} %get-tuple-element.24.refs_2_) | copy-start | bytes 1572868
  24.3 0.9 %copy-start.9 = (bf16[256,512]{1,0:T(8,128)(2,1)}, bf16[256,512]{1,0:T(8,128)(2,1)S(1)}, u32[]{:S(2)}) copy-start(bf16[256,512]{1,0:T(8,128)(2,1)S(1)} %get-tuple-element.17.qt_ref) | copy-start | bytes 786436
  24.4 1.2 %copy-start.11 = (s32[8,12,4,128]{3,2,1,0:T(4,128)S(1)}, s32[8,12,4,128]{3,2,1,0:T(4,128)}, u32[]{:S(2)}) copy-start(s32[8,12,4,128]{3,2,1,0:T(4,128)} %bit_ref.3) | copy-start | bytes 589828
  25.3 5.1 %copy-start.2 = (bf16[256,1536]{1,0:T(8,128)(2,1)}, bf16[256,1536]{1,0:T(8,128)(2,1)S(1)}, u32[]{:S(2)}) copy-start(bf16[256,1536]{1,0:T(8,128)(2,1)S(1)} %get-tuple-element.23.vt_ref) | copy-start | bytes 2359300
  25.3 0.7 %copy-start.15 = (s32[8,12]{1,0:T(8,128)S(1)}, s32[8,12]{1,0:T(8,128)}, u32[]{:S(2)}) copy-start(s32[8,12]{1,0:T(8,128)} %id_ref.3) | copy-start | bytes 1156
  26.0 13.1 %copy-start.4 = (bf16[512,512]{1,0:T(8,128)(2,1)S(1)}, bf16[512,512]{1,0:T(8,128)(2,1)}, u32[]{:S(2)}) copy-start(bf16[512,512]{1,0:T(8,128)(2,1)} %refs_3_.3) | copy-start | bytes 1572868
  30.3 8.8 %collective-permute-start.8 = (bf16[256,256]{1,0:T(8,128)(2,1)}, bf16[256,256]{1,0:T(8,128)(2,1)}, u32[]{:S(2)}, u32[]{:S(2)}) collective-permute-start(bf16[256,256]{1,0:T(8,128)(2,1)} %attend.2.refs_0_), channel_id=1, source_target_pairs={{0,2},{2,0},{1,3},{3,1},{4,6},{6,4},{5,7},{7,5},{8,10},{10,8},{9,1... | collective-permute-start | bytes 393224 | tf_op jit(solution)/shard_map/ppermute | solution.py:322
  30.9 1.1 %copy-start.3 = (bf16[256,1536]{1,0:T(8,128)(2,1)S(1)}, bf16[256,1536]{1,0:T(8,128)(2,1)}, u32[]{:S(2)}) copy-start(bf16[256,1536]{1,0:T(8,128)(2,1)} %copy-done.2) | copy-start | bytes 2359300
  32.0 0.9 %copy-start.10 = (bf16[256,512]{1,0:T(8,128)(2,1)S(1)}, bf16[256,512]{1,0:T(8,128)(2,1)}, u32[]{:S(2)}) copy-start(bf16[256,512]{1,0:T(8,128)(2,1)} %copy-done.9) | copy-start | bytes 786436
  32.9 0.9 %copy-start.12 = (s32[8,12,4,128]{3,2,1,0:T(4,128)S(1)}, s32[8,12,4,128]{3,2,1,0:T(4,128)}, u32[]{:S(2)}) copy-start(s32[8,12,4,128]{3,2,1,0:T(4,128)} %bit_ref.3) | copy-start | bytes 589828
  33.9 5.3 %copy-start = (bf16[1024,512]{1,0:T(8,128)(2,1)S(1)}, bf16[1024,512]{1,0:T(8,128)(2,1)}, u32[]{:S(2)}) copy-start(bf16[1024,512]{1,0:T(8,128)(2,1)} %refs_6_.5) | copy-start | bytes 3145732
  33.9 5.3 %copy-start.1 = (bf16[1024,512]{1,0:T(8,128)(2,1)S(1)}, bf16[1024,512]{1,0:T(8,128)(2,1)}, u32[]{:S(2)}) copy-start(bf16[1024,512]{1,0:T(8,128)(2,1)} %refs_7_.5) | copy-start | bytes 3145732
  37.6 6.0 %collective-permute-start.11 = (bf16[256,256]{1,0:T(8,128)(2,1)S(1)}, bf16[256,256]{1,0:T(8,128)(2,1)}, u32[]{:S(2)}, u32[]{:S(2)}) collective-permute-start(bf16[256,256]{1,0:T(8,128)(2,1)S(1)} %attend.3.refs_0_), channel_id=1, source_target_pairs={{0,2},{2,0},{1,3},{3,1},{4,6},{6,4},{5,7},{7,5},{8,10},{10,8},{9,1... | collective-permute-start | bytes 393224 | tf_op jit(solution)/shard_map/ppermute | solution.py:322
  39.1 1.0 %copy-start.6 = (bf16[512,512]{1,0:T(8,128)(2,1)S(1)}, bf16[512,512]{1,0:T(8,128)(2,1)}, u32[]{:S(2)}) copy-start(bf16[512,512]{1,0:T(8,128)(2,1)} %copy-done.5) | copy-start | bytes 1572868
  43.0 6.3 %collective-permute-start.9 = (bf16[256,256]{1,0:T(8,128)(2,1)}, bf16[256,256]{1,0:T(8,128)(2,1)}, u32[]{:S(2)}, u32[]{:S(2)}) collective-permute-start(bf16[256,256]{1,0:T(8,128)(2,1)} %get-tuple-element.26), channel_id=1, source_target_pairs={{0,2},{2,0},{1,3},{3,1},{4,6},{6,4},{5,7},{7,5},{8,10},{10,8},{9,1... | collective-permute-start | bytes 393224 | tf_op jit(solution)/shard_map/ppermute | solution.py:322
  45.7 5.7 %collective-permute-start.12 = (bf16[256,256]{1,0:T(8,128)(2,1)S(1)}, bf16[256,256]{1,0:T(8,128)(2,1)S(1)}, u32[]{:S(2)}, u32[]{:S(2)}) collective-permute-start(bf16[256,256]{1,0:T(8,128)(2,1)S(1)} %get-tuple-element.28), channel_id=1, source_target_pairs={{0,2},{2,0},{1,3},{3,1},{4,6},{6,4},{5,7},{7,5},{8,10},{10,8},{9,1... | collective-permute-start | bytes 393224 | tf_op jit(solution)/shard_map/ppermute | solution.py:322
  50.3 1.3 %collective-permute-start.10 = (bf16[256,128]{1,0:T(8,128)(2,1)S(1)}, bf16[256,128]{1,0:T(8,128)(2,1)S(1)}, u32[]{:S(2)}, u32[]{:S(2)}) collective-permute-start(bf16[256,128]{1,0:T(8,128)(2,1)S(1)} %broadcast_select_fusion.6), channel_id=1, source_target_pairs={{0,1},{1,0},{2,3},{3,2},{4,5},{5,4},{6,7},{7,6},{8,9},{9,8},{10,11... | collective-permute-start | bytes 196616 | tf_op jit(solution)/shard_map/ppermute | solution.py:322
  51.5 1.3 %collective-permute-start.13 = (bf16[256,128]{1,0:T(8,128)(2,1)S(1)}, bf16[256,128]{1,0:T(8,128)(2,1)S(1)}, u32[]{:S(2)}, u32[]{:S(2)}) collective-permute-start(bf16[256,128]{1,0:T(8,128)(2,1)S(1)} %broadcast_select_fusion.3), channel_id=1, source_target_pairs={{0,1},{1,0},{2,3},{3,2},{4,5},{5,4},{6,7},{7,6},{8,9},{9,8},{10,11... | collective-permute-start | bytes 196616 | tf_op jit(solution)/shard_map/ppermute | solution.py:322

commit v3 on v2

--- a/solution.py
+++ b/solution.py
@@ -43,7 +43,28 @@
 
 def pick_rows(send_list, source):
     shape = jax.ShapeDtypeStruct((send_list.shape[1], source.shape[1]), source.dtype)
-    return pl.pallas_call(pick_body, out_shape=(shape, shape), name="pick_rows")(send_list, source)
+    wide = jax.ShapeDtypeStruct((source.shape[0], 4 * shape.shape[0]), F32)
+    return pl.pallas_call(
+        pick_body,
+        out_shape=(shape, shape),
+        compiler_params=pltpu.CompilerParams(vmem_limit_bytes=vmem_limit(wide, source)),
+        name="pick_rows",
+    )(send_list, source)
+
+
+def flip_body(a_ref, b_ref, at_ref, bt_ref):
+    at_ref[...] = a_ref[...].T
+    bt_ref[...] = b_ref[...].T
+
+
+def flip(a, b):
+    shape = jax.ShapeDtypeStruct(a.shape[::-1], a.dtype)
+    return pl.pallas_call(
+        flip_body,
+        out_shape=(shape, shape),
+        compiler_params=pltpu.CompilerParams(vmem_limit_bytes=vmem_limit(a, b, shape, shape)),
+        name="flip",
+    )(a, b)
 
 
 def vmem_limit(*shapes):
@@ -158,12 +179,38 @@
     first, per_sub, blocks_own, sub_ref, live_ref, id_ref, qt_ref, bit_ref, k_ref, vt_ref,
     out_ref, s_ref,
 ):
+    tile = bit_ref.shape[-1]
+    count = out_ref.shape[0] // tile
+    slots = s_ref.shape[0]
+
+    def step(j, carry):
+        for i in range(slots):
+            attend_block(
+                first, per_sub, blocks_own, j * slots + i, sub_ref, live_ref, id_ref, qt_ref,
+                bit_ref, k_ref, vt_ref, out_ref, s_ref.at[i],
+            )
+        return carry
+
+    if count == slots:
+        step(0, 0)
+    else:
+        lax.fori_loop(0, count // slots, step, 0)
+
+
+def attend_block(
+    first, per_sub, blocks_own, at, sub_ref, live_ref, id_ref, qt_ref, bit_ref, k_ref, vt_ref,
+    out_ref, s_ref,
+):
     slot_count, word_count, tile = bit_ref.shape[1:]
     head_cols = qt_ref.shape[0]
     heads = head_cols // HD
-    block = sub_ref[0] * per_sub + first + pl.program_id(0)
+    block = sub_ref[0] * per_sub + first + at
     live = live_ref[0]
-    qt = qt_ref[...]
+    q_at = (first + at) * tile
+    out_at = at * tile
+    if not isinstance(at, int):
+        q_at, out_at = pl.multiple_of(q_at, tile), pl.multiple_of(out_at, tile)
+    qt = qt_ref[:, pl.ds(q_at, tile)]
     row = lax.broadcasted_iota(jnp.int32, (head_cols, tile), 0)
     spread = jnp.concatenate(
         [jnp.where(row // HD == h, qt, jnp.zeros_like(qt)) for h in range(heads)], axis=1
@@ -188,7 +235,7 @@
             words = jnp.concatenate(
                 [
                     jnp.right_shift(
-                        jnp.broadcast_to(bit_ref[0, t, w : w + 1, :], (per_word, tile)), bit_at
+                        jnp.broadcast_to(bit_ref[block, t, w : w + 1, :], (per_word, tile)), bit_at
                     )
                     & 1
                     for w in range(word_count)
@@ -227,36 +274,27 @@
         g, i = divmod(h, group)
         own = mixed[g][i * HD : (i + 1) * HD, i * tile : (i + 1) * tile]
         pieces.append(own / total[:, h * tile : (h + 1) * tile])
-    out_ref[...] = jnp.concatenate(pieces, axis=0).T.astype(BF16)
+    out_ref[pl.ds(out_at, tile), :] = jnp.concatenate(pieces, axis=0).T.astype(BF16)
 
 
 def attend(sub_id, live_counts, tile_keys, queries_t, tile_bits, keys, values_t, first, count):
-    blocks_own, slot_count, word_count, tile = tile_bits.shape
+    blocks_own, slot_count, _, tile = tile_bits.shape
     head_cols, here = queries_t.shape
-    total = keys.shape[0]
     per_sub = here // tile
     heads = head_cols // HD
-    scratch = jax.ShapeDtypeStruct((slot_count * tile, heads * tile), F32)
+    scratch = jax.ShapeDtypeStruct((math.gcd(count, 2), slot_count * tile, heads * tile), F32)
+    vmem = pl.BlockSpec(memory_space=pltpu.VMEM)
+    smem = pl.BlockSpec(memory_space=pltpu.SMEM)
+    out = jax.ShapeDtypeStruct((count * tile, head_cols), BF16)
+    bits = jax.ShapeDtypeStruct((blocks_own, slot_count, 8, tile), jnp.int32)
     return pl.pallas_call(
         functools.partial(attend_body, first, per_sub, blocks_own),
-        out_shape=jax.ShapeDtypeStruct((count * tile, head_cols), BF16),
-        grid_spec=pltpu.PrefetchScalarGridSpec(
-            num_scalar_prefetch=3,
-            grid=(count,),
-            in_specs=[
-                pl.BlockSpec((head_cols, tile), lambda i, m, n, k: (0, first + i)),
-                pl.BlockSpec(
-                    (1, slot_count, word_count, tile),
-                    lambda i, m, n, k: (m[0] * per_sub + first + i, 0, 0, 0),
-                ),
-                pl.BlockSpec((total, head_cols), lambda i, m, n, k: (0, 0)),
-                pl.BlockSpec((head_cols, total), lambda i, m, n, k: (0, 0)),
-            ],
-            out_specs=pl.BlockSpec((tile, head_cols), lambda i, m, n, k: (i, 0)),
-            scratch_shapes=[pltpu.VMEM(scratch.shape, F32)],
-        ),
+        out_shape=out,
+        in_specs=[smem] * 3 + [vmem] * 4,
+        out_specs=vmem,
+        scratch_shapes=[pltpu.VMEM(scratch.shape, F32)],
         compiler_params=pltpu.CompilerParams(
-            vmem_limit_bytes=vmem_limit(scratch, scratch, keys, keys, values_t, values_t)
+            vmem_limit_bytes=vmem_limit(scratch, keys, values_t, queries_t, bits, out)
         ),
         name="attend",
     )(sub_id, live_counts, tile_keys, queries_t, tile_bits, keys, values_t)
@@ -360,13 +398,19 @@
     upper = lax.ppermute(downward, "space", down)
     halo = jnp.concatenate([lower, upper], axis=0)
     if paired:
-        halo_across = swap(halo, "chan")
-        halos = [halo, swap(halo, "sub"), halo_across, swap(halo_across, "sub")]
+        cross_up = [(2 * i + c, 2 * j + 1 - c) for i, j in up for c in range(2)]
+        cross_down = [(2 * i + c, 2 * j + 1 - c) for i, j in down for c in range(2)]
+        lower = lax.ppermute(upward, ("space", "chan"), cross_up)
+        upper = lax.ppermute(downward, ("space", "chan"), cross_down)
+        halo_across = jnp.concatenate([lower, upper], axis=0)
+        halo_beside = swap(halo, "sub")
+        halo_diagonal = swap(halo_across, "sub")
+        halos = [halo, halo_beside, halo_across, halo_diagonal]
     else:
         halos = [lax.all_gather(halo, ("chan", "sub"), axis=1, tiled=True)]
-    values_w = value_weight.T
+    queries_w, values_w = flip(query_weight, value_weight)
     queries_t, keys, values_t, own_x = project(
-        place, mains, norm_gains, norm_shifts, query_weight.T, key_weight, values_w, here
+        place, mains, norm_gains, norm_shifts, queries_w, key_weight, values_w, here
     )
     keys, values_t = extend(
         place, halos, norm_gains, norm_shifts, key_weight, values_w, keys, values_t

time: 54.1 us -> 55.3 us (1.022)
  starting transfers between devices: 12.8 us -> 17.6 us
  waiting for transfers between devices: 14 us -> 10 us
    ppermute x0 -> x2, starting transfers between devices: none -> 4.74 us  [the longest x1 3.44 us: on_device(): lower = lax.ppermute(upward, ('space', 'chan'), cross_up)]
    ppermute x12 -> x11, waiting for transfers between devices: 8.77 us -> 4.23 us  [swap(): return lax.ppermute(array, axis, [(0, 1), (1, 0)])]
    ppermute x0 -> x2, waiting for transfers between devices: none -> 2.26 us  [the longest x1 2.26 us: on_device(): upper = lax.ppermute(downward, ('space', 'chan'), cross_down)]
    ppermute x12 -> x11, starting transfers between devices: 8.04 us -> 6.52 us  [swap(): return lax.ppermute(array, axis, [(0, 1), (1, 0)])]
    ppermute x1, starting transfers between devices: 3.47 us -> 4.96 us  [on_device(): lower = lax.ppermute(upward, 'space', up)]
    pallas_call x1, Pallas kernels: 1.48 us -> 2.44 us  [project(): pl.pallas_call(functools.partial(project_body, math.gcd(rows, 256), len(m...]
    ppermute x1, waiting for transfers between devices: 4.38 us -> 3.53 us  [on_device(): upper = lax.ppermute(downward, 'space', down)]
    ppermute x1, waiting for transfers between devices: 0.81 us -> 0.01 us  [on_device(): lower = lax.ppermute(upward, 'space', up)]
  transfers between devices with their start and end apart: 14 -> 15, of which waited for: 6 -> 5; matrix products, arithmetic and copies ran while one was open for 3% -> 2% of each run, Pallas kernels for 23% -> 20%
where the time goes in v3:
time: 55.3 us; the launch traced here: 54.7 us
  starting transfers between devices  17.6 us (32%)
  Pallas kernels  17.1 us (31%)
  waiting for transfers between devices  10 us (18%)
  local copies, waits for them, and re-layouts  7.02 us (13%)
  other arithmetic  1.9 us (3%)
  between operations  0.99 us (2%)
    pallas_call x2, Pallas kernels, attend(): pl.pallas_call(functools.partial(attend_body, first, per_sub, blocks_own)...  7.28 us
    unnamed x38, local copies, waits for them, and re-layouts  6.99 us
    ppermute x11, starting transfers between devices, swap(): return lax.ppermute(array, axis, [(0, 1), (1, 0)])  6.52 us
    ppermute x1, starting transfers between devices, on_device(): lower = lax.ppermute(upward, 'space', up)  4.96 us
    pallas_call x2, Pallas kernels, feed(): pl.pallas_call(functools.partial(feed_body, first_row, math.gcd(here, 256...  4.91 us
    ppermute x11, waiting for transfers between devices, swap(): return lax.ppermute(array, axis, [(0, 1), (1, 0)])  4.23 us
    ppermute x1, waiting for transfers between devices, on_device(): upper = lax.ppermute(downward, 'space', down)  3.53 us
    ppermute x1, starting transfers between devices, on_device(): lower = lax.ppermute(upward, ('space', 'chan'), cross_up)  3.44 us
  transfers between devices with their start and end apart: 15, of which 5 were waited for; matrix products, arithmetic and copies ran while one was open for 2% of the time, Pallas kernels for 20%

profile of v3, /device:TPU:0, one launch (start us, length us, event | category | flops | bytes accessed | tf_op | source)
XLA Modules:
  0.0 54.7 jit_solution(461131203807948475)
XLA Ops:
  0.0 0.7 %copy-done.17 = s32[1,2,256]{2,1,0:T(2,128)S(1)} copy-done((s32[1,2,256]{2,1,0:T(2,128)S(1)}, s32[1,2,256]{2,1,0:T(2,128)}, u32[]{:S(2)}) %copy-start.17) | copy-done | bytes 2072
  0.7 1.4 %pick_rows.1 = (bf16[256,128]{1,0:T(8,128)(2,1)S(1)}, bf16[256,128]{1,0:T(8,128)(2,1)S(1)}) custom-call(s32[2,256]{1,0:T(2,128)S(1)} %bitcast.6, bf16[1024,128]{1,0:T(8,128)(2,1)} %x_ref.1), custom_call_target="tpu_custom_call" | custom-call | tf_op jit(solution)/shard_map/pick_rows/pallas_call | solution.py:47
  2.1 5.0 %collective-permute-start.3 = (bf16[256,128]{1,0:T(8,128)(2,1)S(1)}, bf16[256,128]{1,0:T(8,128)(2,1)S(1)}, u32[]{:S(2)}, u32[]{:S(2)}) collective-permute-start(bf16[256,128]{1,0:T(8,128)(2,1)S(1)} %get-tuple-element.22), channel_id=1, source_target_pairs={{0,4},{4,8},{8,12},{1,5},{5,9},{9,13},{2,6},{6,10},{10,14},{3,7},{... | collective-permute-start | bytes 196616 | tf_op jit(solution)/shard_map/ppermute | solution.py:397
  7.1 1.6 %collective-permute-start.1 = (bf16[1024,128]{1,0:T(8,128)(2,1)}, bf16[1024,128]{1,0:T(8,128)(2,1)S(1)}, u32[]{:S(2)}, u32[]{:S(2)}) collective-permute-start(bf16[1024,128]{1,0:T(8,128)(2,1)} %x_ref.1), channel_id=1, source_target_pairs={{0,2},{2,0},{1,3},{3,1},{4,6},{6,4},{5,7},{7,5},{8,10},{10,8},{9,1... | collective-permute-start | bytes 786440 | tf_op jit(solution)/shard_map/ppermute | solution.py:360
  8.6 3.4 %collective-permute-start.6 = (bf16[256,128]{1,0:T(8,128)(2,1)S(1)}, bf16[256,128]{1,0:T(8,128)(2,1)S(1)}, u32[]{:S(2)}, u32[]{:S(2)}) collective-permute-start(bf16[256,128]{1,0:T(8,128)(2,1)S(1)} %get-tuple-element.22), channel_id=1, source_target_pairs={{0,6},{2,4},{4,10},{6,8},{8,14},{10,12},{1,7},{3,5},{5,11},{7,9},{... | collective-permute-start | bytes 196616 | tf_op jit(solution)/shard_map/ppermute | solution.py:403
  12.1 1.4 %collective-permute-start.4 = (bf16[256,128]{1,0:T(8,128)(2,1)S(1)}, bf16[256,128]{1,0:T(8,128)(2,1)S(1)}, u32[]{:S(2)}, u32[]{:S(2)}) collective-permute-start(bf16[256,128]{1,0:T(8,128)(2,1)S(1)} %get-tuple-element.23), channel_id=1, source_target_pairs={{4,0},{8,4},{12,8},{5,1},{9,5},{13,9},{6,2},{10,6},{14,10},{7,3},{... | collective-permute-start | bytes 196616 | tf_op jit(solution)/shard_map/ppermute | solution.py:398
  13.6 1.3 %collective-permute-start.7 = (bf16[256,128]{1,0:T(8,128)(2,1)S(1)}, bf16[256,128]{1,0:T(8,128)(2,1)S(1)}, u32[]{:S(2)}, u32[]{:S(2)}) collective-permute-start(bf16[256,128]{1,0:T(8,128)(2,1)S(1)} %get-tuple-element.23), channel_id=1, source_target_pairs={{4,2},{6,0},{8,6},{10,4},{12,10},{14,8},{5,3},{7,1},{9,7},{11,5},{... | collective-permute-start | bytes 196616 | tf_op jit(solution)/shard_map/ppermute | solution.py:404
  14.9 3.5 %collective-permute-done.4 = bf16[256,128]{1,0:T(8,128)(2,1)S(1)} collective-permute-done((bf16[256,128]{1,0:T(8,128)(2,1)S(1)}, bf16[256,128]{1,0:T(8,128)(2,1)S(1)}, u32[]{:S(2)}, u32[]{:S(2)}) %collective-permute-start.4) | collective-permute-done | bytes 65568 | tf_op jit(solution)/shard_map/ppermute | solution.py:398
  18.5 0.5 collective-permute-start.2
  19.0 2.3 %collective-permute-done.7 = bf16[256,128]{1,0:T(8,128)(2,1)S(1)} collective-permute-done((bf16[256,128]{1,0:T(8,128)(2,1)S(1)}, bf16[256,128]{1,0:T(8,128)(2,1)S(1)}, u32[]{:S(2)}, u32[]{:S(2)}) %collective-permute-start.7) | collective-permute-done | bytes 65568 | tf_op jit(solution)/shard_map/ppermute | solution.py:404
  22.3 0.7 %copy-done.7 = bf16[512,256]{1,0:T(8,128)(2,1)S(1)} copy-done((bf16[512,256]{1,0:T(8,128)(2,1)S(1)}, bf16[512,256]{1,0:T(8,128)(2,1)}, u32[]{:S(2)}) %copy-start.7) | copy-done | bytes 262168
  23.0 2.4 %project.1 = (bf16[256,512]{1,0:T(8,128)(2,1)S(1)}, bf16[1024,256]{1,0:T(8,128)(2,1)S(1)}, bf16[256,1024]{1,0:T(8,128)(2,1)S(1)}, bf16[512,512]{1,0:T(8,128)(2,1)S(1)}) custom-call(s32[1]{0:T(128)} %bitcast.1.chan_ref, s32[1]{0:T(128)} %bitcast.2.sub_ref, bf16[1024,128]{1,0:T(8,128)(2,1)} %x_ref.1, bf16[1024,128]{1,0:T(8,128)(2,1)S(1)} %collective-permute-done.refs_1_, ...), custom_call_target="tpu_custom_call" | custom-call | tf_op jit(solution)/shard_map/project/pallas_call | solution.py:128
  25.5 0.8 %copy-done.5 = bf16[512,512]{1,0:T(8,128)(2,1)} copy-done((bf16[512,512]{1,0:T(8,128)(2,1)}, bf16[512,512]{1,0:T(8,128)(2,1)S(1)}, u32[]{:S(2)}) %copy-start.5) | copy-done | bytes 524312
  26.3 0.9 %extend.1 = (bf16[1536,256]{1,0:T(8,128)(2,1)S(1)}, bf16[256,1536]{1,0:T(8,128)(2,1)S(1)}) custom-call(s32[1]{0:T(128)} %bitcast.1.chan_ref, s32[1]{0:T(128)} %bitcast.2.sub_ref, bf16[512,128]{1,0:T(8,128)(2,1)S(1)} %constant_dynamic-update-slice_fusion.refs_0_, bf16[512,128]{1,0:T(8,128)(2,1)S(1)} %collective-permute-done.5.refs_1_, ...), custom_call_target="tpu_custom_call" | custom-call | tf_op jit(solution)/shard_map/extend/pallas_call | solution.py:165
  27.3 0.6 %copy-done.16 = s32[8,12]{1,0:T(8,128)S(1)} copy-done((s32[8,12]{1,0:T(8,128)S(1)}, s32[8,12]{1,0:T(8,128)}, u32[]{:S(2)}) %copy-start.16) | copy-done | bytes 408
  27.9 4.0 %attend.2.refs_0_ = bf16[256,256]{1,0:T(8,128)(2,1)} custom-call(s32[1]{0:T(128)} %bitcast.2.sub_ref, s32[1]{0:T(128)} %copy.16.live_ref, s32[8,12]{1,0:T(8,128)S(1)} %copy-done.16, bf16[256,512]{1,0:T(8,128)(2,1)S(1)} %get-tuple-element.21.qt_ref, s32[8,12,4,128]{3,2,1,0:T(4,128)S(1)} %copy-done.10, bf16[1536,256]{1,0:T(8,128)(2,1)S(1)} %get-tuple-element.26.k_ref, ...), custom_call_target="tpu_custom_call" | custom-call | tf_op jit(solution)/shard_map/attend/pallas_call | solution.py:290
  31.9 0.8 %collective-permute-start.9 = (bf16[256,256]{1,0:T(8,128)(2,1)}, bf16[256,256]{1,0:T(8,128)(2,1)}, u32[]{:S(2)}, u32[]{:S(2)}) collective-permute-start(bf16[256,256]{1,0:T(8,128)(2,1)} %attend.2.refs_0_), channel_id=1, source_target_pairs={{0,2},{2,0},{1,3},{3,1},{4,6},{6,4},{5,7},{7,5},{8,10},{10,8},{9,1... | collective-permute-start | bytes 393224 | tf_op jit(solution)/shard_map/ppermute | solution.py:360
  32.7 1.1 %copy-done.3 = bf16[256,1536]{1,0:T(8,128)(2,1)S(1)} copy-done((bf16[256,1536]{1,0:T(8,128)(2,1)S(1)}, bf16[256,1536]{1,0:T(8,128)(2,1)}, u32[]{:S(2)}) %copy-start.3) | copy-done | bytes 786456
  33.8 0.9 %copy-done.9 = bf16[256,512]{1,0:T(8,128)(2,1)S(1)} copy-done((bf16[256,512]{1,0:T(8,128)(2,1)S(1)}, bf16[256,512]{1,0:T(8,128)(2,1)}, u32[]{:S(2)}) %copy-start.9) | copy-done | bytes 262168
  34.8 0.9 %copy-done.11 = s32[8,12,4,128]{3,2,1,0:T(4,128)S(1)} copy-done((s32[8,12,4,128]{3,2,1,0:T(4,128)S(1)}, s32[8,12,4,128]{3,2,1,0:T(4,128)}, u32[]{:S(2)}) %copy-start.11) | copy-done | bytes 196632
  35.7 3.3 %attend.3.refs_0_ = bf16[256,256]{1,0:T(8,128)(2,1)S(1)} custom-call(s32[1]{0:T(128)} %bitcast.2.sub_ref, s32[1]{0:T(128)} %copy.16.live_ref, s32[8,12]{1,0:T(8,128)S(1)} %copy-done.16, bf16[256,512]{1,0:T(8,128)(2,1)S(1)} %copy-done.9, s32[8,12,4,128]{3,2,1,0:T(4,128)S(1)} %copy-done.11, bf16[1536,256]{1,0:T(8,128)(2,1)S(1)} %get-tuple-element.26.k_ref, ...), custom_call_target="tpu_custom_call" | custom-call | tf_op jit(solution)/shard_map/attend/pallas_call | solution.py:290
  39.0 1.3 %collective-permute-start.12 = (bf16[256,256]{1,0:T(8,128)(2,1)S(1)}, bf16[256,256]{1,0:T(8,128)(2,1)}, u32[]{:S(2)}, u32[]{:S(2)}) collective-permute-start(bf16[256,256]{1,0:T(8,128)(2,1)S(1)} %attend.3.refs_0_), channel_id=1, source_target_pairs={{0,2},{2,0},{1,3},{3,1},{4,6},{6,4},{5,7},{7,5},{8,10},{10,8},{9,1... | collective-permute-start | bytes 393224 | tf_op jit(solution)/shard_map/ppermute | solution.py:360
  40.3 1.0 %copy-done.6 = bf16[512,512]{1,0:T(8,128)(2,1)S(1)} copy-done((bf16[512,512]{1,0:T(8,128)(2,1)S(1)}, bf16[512,512]{1,0:T(8,128)(2,1)}, u32[]{:S(2)}) %copy-start.6) | copy-done | bytes 524312
  41.3 2.8 %feed.2 = (bf16[256,256]{1,0:T(8,128)(2,1)}, f32[256,256]{1,0:T(8,128)S(1)}) custom-call(s32[1]{0:T(128)} %bitcast.1.chan_ref, bf16[256,256]{1,0:T(8,128)(2,1)} %attend.2.refs_0_, bf16[256,256]{1,0:T(8,128)(2,1)} %collective-permute-done.9.refs_1_, bf16[512,512]{1,0:T(8,128)(2,1)S(1)} %copy-done.6, bf16[512,512]{1,0:T(8,128)(2,1)S(1)} %copy-done.4, ...), custom_call_target="tpu_custom_call" | custom-call | tf_op jit(solution)/shard_map/feed/pallas_call | solution.py:347
  44.2 0.8 %collective-permute-start.10 = (bf16[256,256]{1,0:T(8,128)(2,1)}, bf16[256,256]{1,0:T(8,128)(2,1)}, u32[]{:S(2)}, u32[]{:S(2)}) collective-permute-start(bf16[256,256]{1,0:T(8,128)(2,1)} %get-tuple-element.30), channel_id=1, source_target_pairs={{0,2},{2,0},{1,3},{3,1},{4,6},{6,4},{5,7},{7,5},{8,10},{10,8},{9,1... | collective-permute-start | bytes 393224 | tf_op jit(solution)/shard_map/ppermute | solution.py:360
  45.0 2.1 %feed.3 = (bf16[256,256]{1,0:T(8,128)(2,1)S(1)}, f32[256,256]{1,0:T(8,128)S(1)}) custom-call(s32[1]{0:T(128)} %bitcast.1.chan_ref, bf16[256,256]{1,0:T(8,128)(2,1)S(1)} %attend.3.refs_0_, bf16[256,256]{1,0:T(8,128)(2,1)} %collective-permute-done.12.refs_1_, bf16[512,512]{1,0:T(8,128)(2,1)S(1)} %copy-done.6, bf16[512,512]{1,0:T(8,128)(2,1)S(1)} %copy-done.4, ...), custom_call_target="tpu_custom_call" | custom-call | tf_op jit(solution)/shard_map/feed/pallas_call | solution.py:347
  47.1 1.3 %collective-permute-start.13 = (bf16[256,256]{1,0:T(8,128)(2,1)S(1)}, bf16[256,256]{1,0:T(8,128)(2,1)S(1)}, u32[]{:S(2)}, u32[]{:S(2)}) collective-permute-start(bf16[256,256]{1,0:T(8,128)(2,1)S(1)} %get-tuple-element.32), channel_id=1, source_target_pairs={{0,2},{2,0},{1,3},{3,1},{4,6},{6,4},{5,7},{7,5},{8,10},{10,8},{9,1... | collective-permute-start | bytes 393224 | tf_op jit(solution)/shard_map/ppermute | solution.py:360
  48.4 1.7 %collective-permute-done.10 = bf16[256,256]{1,0:T(8,128)(2,1)} collective-permute-done((bf16[256,256]{1,0:T(8,128)(2,1)}, bf16[256,256]{1,0:T(8,128)(2,1)}, u32[]{:S(2)}, u32[]{:S(2)}) %collective-permute-start.10) | collective-permute-done | bytes 131104 | tf_op jit(solution)/shard_map/ppermute | solution.py:360
  50.1 1.0 %select_convert_fusion.1 = bf16[256,256]{1,0:T(8,128)(2,1)S(1)} fusion(f32[256,256]{1,0:T(8,128)S(1)} %get-tuple-element.29, bf16[256,256]{1,0:T(8,128)(2,1)} %collective-permute-done.10, pred[256]{0:T(512)(128)(4,1)S(1)} %add_compare_fusion.1), kind=kLoop, calls=%fused_computation.2 | loop fusion | flops 262144 | bytes 524544 | tf_op jit(solution)/shard_map/convert_element_type | solution.py:448
  51.2 1.3 %collective-permute-done.13 = bf16[256,256]{1,0:T(8,128)(2,1)S(1)} collective-permute-done((bf16[256,256]{1,0:T(8,128)(2,1)S(1)}, bf16[256,256]{1,0:T(8,128)(2,1)S(1)}, u32[]{:S(2)}, u32[]{:S(2)}) %collective-permute-start.13) | collective-permute-done | bytes 131104 | tf_op jit(solution)/shard_map/ppermute | solution.py:360
  52.7 1.2 %collective-permute-done.14 = bf16[256,128]{1,0:T(8,128)(2,1)S(1)} collective-permute-done((bf16[256,128]{1,0:T(8,128)(2,1)S(1)}, bf16[256,128]{1,0:T(8,128)(2,1)S(1)}, u32[]{:S(2)}, u32[]{:S(2)}) %collective-permute-start.14) | collective-permute-done | bytes 65568 | tf_op jit(solution)/shard_map/ppermute | solution.py:360
  54.0 0.7 %pad_maximum_fusion = bf16[1024,128]{1,0:T(8,128)(2,1)} fusion(bf16[256,128]{1,0:T(8,128)(2,1)S(1)} %get-tuple-element.36, bf16[256,128]{1,0:T(8,128)(2,1)S(1)} %get-tuple-element.34, bf16[256,128]{1,0:T(8,128)(2,1)S(1)} %get-tuple-element.35, bf16[256,128]{1,0:T(8,128)(2,1)S(1)} %get-tuple-element.33), kind=kLoop, calls=%fused_computation | loop fusion | flops 1048576 | bytes 524288 | tf_op jit(solution)/shard_map/concatenate | solution.py:458
  (55 shorter events, 0.9 us)
Async XLA Ops:
  2.1 11.4 %collective-permute-start.3 = (bf16[256,128]{1,0:T(8,128)(2,1)S(1)}, bf16[256,128]{1,0:T(8,128)(2,1)S(1)}, u32[]{:S(2)}, u32[]{:S(2)}) collective-permute-start(bf16[256,128]{1,0:T(8,128)(2,1)S(1)} %get-tuple-element.22), channel_id=1, source_target_pairs={{0,4},{4,8},{8,12},{1,5},{5,9},{9,13},{2,6},{6,10},{10,14},{3,7},{... | collective-permute-start | bytes 196616 | tf_op jit(solution)/shard_map/ppermute | solution.py:397
  7.1 11.4 %collective-permute-start.1 = (bf16[1024,128]{1,0:T(8,128)(2,1)}, bf16[1024,128]{1,0:T(8,128)(2,1)S(1)}, u32[]{:S(2)}, u32[]{:S(2)}) collective-permute-start(bf16[1024,128]{1,0:T(8,128)(2,1)} %x_ref.1), channel_id=1, source_target_pairs={{0,2},{2,0},{1,3},{3,1},{4,6},{6,4},{5,7},{7,5},{8,10},{10,8},{9,1... | collective-permute-start | bytes 786440 | tf_op jit(solution)/shard_map/ppermute | solution.py:360
  8.6 13.6 %collective-permute-start = (bf16[1024,128]{1,0:T(8,128)(2,1)}, bf16[1024,128]{1,0:T(8,128)(2,1)S(1)}, u32[]{:S(2)}, u32[]{:S(2)}) collective-permute-start(bf16[1024,128]{1,0:T(8,128)(2,1)} %x_ref.1), channel_id=1, source_target_pairs={{0,1},{1,0},{2,3},{3,2},{4,5},{5,4},{6,7},{7,6},{8,9},{9,8},{10,11... | collective-permute-start | bytes 786440 | tf_op jit(solution)/shard_map/ppermute | solution.py:360
  8.6 10.4 %collective-permute-start.6 = (bf16[256,128]{1,0:T(8,128)(2,1)S(1)}, bf16[256,128]{1,0:T(8,128)(2,1)S(1)}, u32[]{:S(2)}, u32[]{:S(2)}) collective-permute-start(bf16[256,128]{1,0:T(8,128)(2,1)S(1)} %get-tuple-element.22), channel_id=1, source_target_pairs={{0,6},{2,4},{4,10},{6,8},{8,14},{10,12},{1,7},{3,5},{5,11},{7,9},{... | collective-permute-start | bytes 196616 | tf_op jit(solution)/shard_map/ppermute | solution.py:403
  12.1 9.9 %copy-start.12 = (bf16[512,256]{1,0:T(8,128)(2,1)S(1)}, bf16[512,256]{1,0:T(8,128)(2,1)}, u32[]{:S(2)}) copy-start(bf16[512,256]{1,0:T(8,128)(2,1)} %a_ref.1) | copy-start | bytes 786436
  12.1 9.9 %copy-start.13 = (bf16[512,256]{1,0:T(8,128)(2,1)S(1)}, bf16[512,256]{1,0:T(8,128)(2,1)}, u32[]{:S(2)}) copy-start(bf16[512,256]{1,0:T(8,128)(2,1)} %b_ref.1) | copy-start | bytes 786436
  12.1 6.3 %collective-permute-start.4 = (bf16[256,128]{1,0:T(8,128)(2,1)S(1)}, bf16[256,128]{1,0:T(8,128)(2,1)S(1)}, u32[]{:S(2)}, u32[]{:S(2)}) collective-permute-start(bf16[256,128]{1,0:T(8,128)(2,1)S(1)} %get-tuple-element.23), channel_id=1, source_target_pairs={{4,0},{8,4},{12,8},{5,1},{9,5},{13,9},{6,2},{10,6},{14,10},{7,3},{... | collective-permute-start | bytes 196616 | tf_op jit(solution)/shard_map/ppermute | solution.py:398
  13.6 7.7 %collective-permute-start.7 = (bf16[256,128]{1,0:T(8,128)(2,1)S(1)}, bf16[256,128]{1,0:T(8,128)(2,1)S(1)}, u32[]{:S(2)}, u32[]{:S(2)}) collective-permute-start(bf16[256,128]{1,0:T(8,128)(2,1)S(1)} %get-tuple-element.23), channel_id=1, source_target_pairs={{4,2},{6,0},{8,6},{10,4},{12,10},{14,8},{5,3},{7,1},{9,7},{11,5},{... | collective-permute-start | bytes 196616 | tf_op jit(solution)/shard_map/ppermute | solution.py:404
  18.4 7.8 %collective-permute-start.5 = (bf16[512,128]{1,0:T(8,128)(2,1)S(1)}, bf16[512,128]{1,0:T(8,128)(2,1)S(1)}, u32[]{:S(2)}, u32[]{:S(2)}) collective-permute-start(bf16[512,128]{1,0:T(8,128)(2,1)S(1)} %constant_dynamic-update-slice_fusion.refs_0_), channel_id=1, source_target_pairs={{0,1},{1,0},{2,3},{3,2},{4,5},{5,4},{6,7},{7,6},{8,9},{9,8},{10,11... | collective-permute-start | bytes 393224 | tf_op jit(solution)/shard_map/ppermute | solution.py:360
  18.5 3.8 %collective-permute-start.2 = (bf16[1024,128]{1,0:T(8,128)(2,1)S(1)}, bf16[1024,128]{1,0:T(8,128)(2,1)S(1)}, u32[]{:S(2)}, u32[]{:S(2)}) collective-permute-start(bf16[1024,128]{1,0:T(8,128)(2,1)S(1)} %collective-permute-done.1.refs_2_), channel_id=1, source_target_pairs={{0,1},{1,0},{2,3},{3,2},{4,5},{5,4},{6,7},{7,6},{8,9},{9,8},{10,11... | collective-permute-start | bytes 786440 | tf_op jit(solution)/shard_map/ppermute | solution.py:360
  21.3 5.0 %collective-permute-start.8 = (bf16[512,128]{1,0:T(8,128)(2,1)S(1)}, bf16[512,128]{1,0:T(8,128)(2,1)S(1)}, u32[]{:S(2)}, u32[]{:S(2)}) collective-permute-start(bf16[512,128]{1,0:T(8,128)(2,1)S(1)} %constant_dynamic-update-slice_fusion.2.refs_2_), channel_id=1, source_target_pairs={{0,1},{1,0},{2,3},{3,2},{4,5},{5,4},{6,7},{7,6},{8,9},{9,8},{10,11... | collective-permute-start | bytes 393224 | tf_op jit(solution)/shard_map/ppermute | solution.py:360
  22.0 1.0 %copy-start.7 = (bf16[512,256]{1,0:T(8,128)(2,1)S(1)}, bf16[512,256]{1,0:T(8,128)(2,1)}, u32[]{:S(2)}) copy-start(bf16[512,256]{1,0:T(8,128)(2,1)} %refs_6_.3) | copy-start | bytes 786436
  22.1 0.9 %copy-start.15 = (f32[2,512]{1,0:T(2,128)S(1)}, f32[2,512]{1,0:T(2,128)}, u32[]{:S(2)}) copy-start(f32[2,512]{1,0:T(2,128)} %refs_5_.7) | copy-start | bytes 12292
  22.3 0.7 %copy-start.14 = (f32[2,512]{1,0:T(2,128)S(1)}, f32[2,512]{1,0:T(2,128)}, u32[]{:S(2)}) copy-start(f32[2,512]{1,0:T(2,128)} %refs_4_.7) | copy-start | bytes 12292
  25.5 0.8 %copy-start.5 = (bf16[512,512]{1,0:T(8,128)(2,1)}, bf16[512,512]{1,0:T(8,128)(2,1)S(1)}, u32[]{:S(2)}) copy-start(bf16[512,512]{1,0:T(8,128)(2,1)S(1)} %get-tuple-element.28.refs_2_) | copy-start | bytes 1572868
  26.2 0.9 %copy-start.8 = (bf16[256,512]{1,0:T(8,128)(2,1)}, bf16[256,512]{1,0:T(8,128)(2,1)S(1)}, u32[]{:S(2)}) copy-start(bf16[256,512]{1,0:T(8,128)(2,1)S(1)} %get-tuple-element.21.qt_ref) | copy-start | bytes 786436
  26.3 1.0 %copy-start.10 = (s32[8,12,4,128]{3,2,1,0:T(4,128)S(1)}, s32[8,12,4,128]{3,2,1,0:T(4,128)}, u32[]{:S(2)}) copy-start(s32[8,12,4,128]{3,2,1,0:T(4,128)} %bit_ref.3) | copy-start | bytes 589828
  27.1 4.7 %copy-start.2 = (bf16[256,1536]{1,0:T(8,128)(2,1)}, bf16[256,1536]{1,0:T(8,128)(2,1)S(1)}, u32[]{:S(2)}) copy-start(bf16[256,1536]{1,0:T(8,128)(2,1)S(1)} %get-tuple-element.27.vt_ref) | copy-start | bytes 2359300
  27.1 0.7 %copy-start.16 = (s32[8,12]{1,0:T(8,128)S(1)}, s32[8,12]{1,0:T(8,128)}, u32[]{:S(2)}) copy-start(s32[8,12]{1,0:T(8,128)} %id_ref.3) | copy-start | bytes 1156
  27.9 12.4 %copy-start.4 = (bf16[512,512]{1,0:T(8,128)(2,1)S(1)}, bf16[512,512]{1,0:T(8,128)(2,1)}, u32[]{:S(2)}) copy-start(bf16[512,512]{1,0:T(8,128)(2,1)} %refs_3_.3) | copy-start | bytes 1572868
  31.9 8.4 %collective-permute-start.9 = (bf16[256,256]{1,0:T(8,128)(2,1)}, bf16[256,256]{1,0:T(8,128)(2,1)}, u32[]{:S(2)}, u32[]{:S(2)}) collective-permute-start(bf16[256,256]{1,0:T(8,128)(2,1)} %attend.2.refs_0_), channel_id=1, source_target_pairs={{0,2},{2,0},{1,3},{3,1},{4,6},{6,4},{5,7},{7,5},{8,10},{10,8},{9,1... | collective-permute-start | bytes 393224 | tf_op jit(solution)/shard_map/ppermute | solution.py:360
  32.7 1.1 %copy-start.3 = (bf16[256,1536]{1,0:T(8,128)(2,1)S(1)}, bf16[256,1536]{1,0:T(8,128)(2,1)}, u32[]{:S(2)}) copy-start(bf16[256,1536]{1,0:T(8,128)(2,1)} %copy-done.2) | copy-start | bytes 2359300
  33.8 0.9 %copy-start.9 = (bf16[256,512]{1,0:T(8,128)(2,1)S(1)}, bf16[256,512]{1,0:T(8,128)(2,1)}, u32[]{:S(2)}) copy-start(bf16[256,512]{1,0:T(8,128)(2,1)} %copy-done.8) | copy-start | bytes 786436
  34.8 0.9 %copy-start.11 = (s32[8,12,4,128]{3,2,1,0:T(4,128)S(1)}, s32[8,12,4,128]{3,2,1,0:T(4,128)}, u32[]{:S(2)}) copy-start(s32[8,12,4,128]{3,2,1,0:T(4,128)} %bit_ref.3) | copy-start | bytes 589828
  35.7 4.6 %copy-start = (bf16[1024,512]{1,0:T(8,128)(2,1)S(1)}, bf16[1024,512]{1,0:T(8,128)(2,1)}, u32[]{:S(2)}) copy-start(bf16[1024,512]{1,0:T(8,128)(2,1)} %refs_6_.5) | copy-start | bytes 3145732
  35.7 4.6 %copy-start.1 = (bf16[1024,512]{1,0:T(8,128)(2,1)S(1)}, bf16[1024,512]{1,0:T(8,128)(2,1)}, u32[]{:S(2)}) copy-start(bf16[1024,512]{1,0:T(8,128)(2,1)} %refs_7_.5) | copy-start | bytes 3145732
  39.0 6.0 %collective-permute-start.12 = (bf16[256,256]{1,0:T(8,128)(2,1)S(1)}, bf16[256,256]{1,0:T(8,128)(2,1)}, u32[]{:S(2)}, u32[]{:S(2)}) collective-permute-start(bf16[256,256]{1,0:T(8,128)(2,1)S(1)} %attend.3.refs_0_), channel_id=1, source_target_pairs={{0,2},{2,0},{1,3},{3,1},{4,6},{6,4},{5,7},{7,5},{8,10},{10,8},{9,1... | collective-permute-start | bytes 393224 | tf_op jit(solution)/shard_map/ppermute | solution.py:360
  40.3 1.0 %copy-start.6 = (bf16[512,512]{1,0:T(8,128)(2,1)S(1)}, bf16[512,512]{1,0:T(8,128)(2,1)}, u32[]{:S(2)}) copy-start(bf16[512,512]{1,0:T(8,128)(2,1)} %copy-done.5) | copy-start | bytes 1572868
  44.2 5.9 %collective-permute-start.10 = (bf16[256,256]{1,0:T(8,128)(2,1)}, bf16[256,256]{1,0:T(8,128)(2,1)}, u32[]{:S(2)}, u32[]{:S(2)}) collective-permute-start(bf16[256,256]{1,0:T(8,128)(2,1)} %get-tuple-element.30), channel_id=1, source_target_pairs={{0,2},{2,0},{1,3},{3,1},{4,6},{6,4},{5,7},{7,5},{8,10},{10,8},{9,1... | collective-permute-start | bytes 393224 | tf_op jit(solution)/shard_map/ppermute | solution.py:360
  47.1 5.4 %collective-permute-start.13 = (bf16[256,256]{1,0:T(8,128)(2,1)S(1)}, bf16[256,256]{1,0:T(8,128)(2,1)S(1)}, u32[]{:S(2)}, u32[]{:S(2)}) collective-permute-start(bf16[256,256]{1,0:T(8,128)(2,1)S(1)} %get-tuple-element.32), channel_id=1, source_target_pairs={{0,2},{2,0},{1,3},{3,1},{4,6},{6,4},{5,7},{7,5},{8,10},{10,8},{9,1... | collective-permute-start | bytes 393224 | tf_op jit(solution)/shard_map/ppermute | solution.py:360
  51.1 1.6 %collective-permute-start.11 = (bf16[256,128]{1,0:T(8,128)(2,1)S(1)}, bf16[256,128]{1,0:T(8,128)(2,1)S(1)}, u32[]{:S(2)}, u32[]{:S(2)}) collective-permute-start(bf16[256,128]{1,0:T(8,128)(2,1)S(1)} %broadcast_select_fusion.6), channel_id=1, source_target_pairs={{0,1},{1,0},{2,3},{3,2},{4,5},{5,4},{6,7},{7,6},{8,9},{9,8},{10,11... | collective-permute-start | bytes 196616 | tf_op jit(solution)/shard_map/ppermute | solution.py:360
  52.6 1.3 %collective-permute-start.14 = (bf16[256,128]{1,0:T(8,128)(2,1)S(1)}, bf16[256,128]{1,0:T(8,128)(2,1)S(1)}, u32[]{:S(2)}, u32[]{:S(2)}) collective-permute-start(bf16[256,128]{1,0:T(8,128)(2,1)S(1)} %broadcast_select_fusion.3), channel_id=1, source_target_pairs={{0,1},{1,0},{2,3},{3,2},{4,5},{5,4},{6,7},{7,6},{8,9},{9,8},{10,11... | collective-permute-start | bytes 196616 | tf_op jit(solution)/shard_map/ppermute | solution.py:360
  (1 other events, 0.7 us)

commit v4 on v3

--- a/solution.py
+++ b/solution.py
@@ -398,11 +398,7 @@
     upper = lax.ppermute(downward, "space", down)
     halo = jnp.concatenate([lower, upper], axis=0)
     if paired:
-        cross_up = [(2 * i + c, 2 * j + 1 - c) for i, j in up for c in range(2)]
-        cross_down = [(2 * i + c, 2 * j + 1 - c) for i, j in down for c in range(2)]
-        lower = lax.ppermute(upward, ("space", "chan"), cross_up)
-        upper = lax.ppermute(downward, ("space", "chan"), cross_down)
-        halo_across = jnp.concatenate([lower, upper], axis=0)
+        halo_across = swap(halo, "chan")
         halo_beside = swap(halo, "sub")
         halo_diagonal = swap(halo_across, "sub")
         halos = [halo, halo_beside, halo_across, halo_diagonal]

time: 55.3 us -> 54.1 us (0.978)
  starting transfers between devices: 17.6 us -> 12.8 us
  waiting for transfers between devices: 10 us -> 13.7 us
    ppermute x2 -> x0, starting transfers between devices: 4.74 us -> none  [the longest x1 3.44 us: on_device(): lower = lax.ppermute(upward, ('space', 'chan'), cross_up)]
    ppermute x11 -> x12, waiting for transfers between devices: 4.23 us -> 8.74 us  [swap(): return lax.ppermute(array, axis, [(0, 1), (1, 0)])]
    ppermute x2 -> x0, waiting for transfers between devices: 2.26 us -> none  [the longest x1 2.26 us: on_device(): upper = lax.ppermute(downward, ('space', 'chan'), cross_down)]
    ppermute x11 -> x12, starting transfers between devices: 6.52 us -> 8.04 us  [swap(): return lax.ppermute(array, axis, [(0, 1), (1, 0)])]
    ppermute x1, starting transfers between devices: 4.96 us -> 3.48 us  [on_device(): lower = lax.ppermute(upward, 'space', up)]
    ppermute x1, waiting for transfers between devices: 3.53 us -> 4.48 us  [on_device(): upper = lax.ppermute(downward, 'space', down)]
    unnamed x38 -> x37, local copies, waits for them, and re-layouts: 6.99 us -> 6.99 us
  transfers between devices with their start and end apart: 15 -> 14, of which waited for: 5 -> 6; matrix products, arithmetic and copies ran while one was open for 2% -> 2% of each run, Pallas kernels for 20% -> 23%
where the time goes in v4:
time: 54.1 us; the launch traced here: 53.5 us
  Pallas kernels  17.2 us (32%)
  waiting for transfers between devices  13.7 us (25%)
  starting transfers between devices  12.8 us (24%)
  local copies, waits for them, and re-layouts  7.01 us (13%)
  other arithmetic  1.9 us (4%)
  between operations  0.93 us (2%)
    ppermute x12, waiting for transfers between devices, swap(): return lax.ppermute(array, axis, [(0, 1), (1, 0)])  8.74 us
    ppermute x12, starting transfers between devices, swap(): return lax.ppermute(array, axis, [(0, 1), (1, 0)])  8.04 us
    pallas_call x2, Pallas kernels, attend(): pl.pallas_call(functools.partial(attend_body, first, per_sub, blocks_own)...  7.28 us
    unnamed x37, local copies, waits for them, and re-layouts  6.99 us
    pallas_call x2, Pallas kernels, feed(): pl.pallas_call(functools.partial(feed_body, first_row, math.gcd(here, 256...  4.91 us
    ppermute x1, waiting for transfers between devices, on_device(): upper = lax.ppermute(downward, 'space', down)  4.48 us
    ppermute x1, starting transfers between devices, on_device(): lower = lax.ppermute(upward, 'space', up)  3.48 us
    pallas_call x1, Pallas kernels, project(): pl.pallas_call(functools.partial(project_body, math.gcd(rows, 256), len(m...  2.44 us
  transfers between devices with their start and end apart: 14, of which 6 were waited for; matrix products, arithmetic and copies ran while one was open for 2% of the time, Pallas kernels for 23%

profile of v4, /device:TPU:0, one launch (start us, length us, event | category | flops | bytes accessed | tf_op | source)
XLA Modules:
  0.0 53.5 jit_solution(2569618835093343237)
XLA Ops:
  0.0 3.0 %collective-permute-start.1 = (bf16[1024,128]{1,0:T(8,128)(2,1)}, bf16[1024,128]{1,0:T(8,128)(2,1)S(1)}, u32[]{:S(2)}, u32[]{:S(2)}) collective-permute-start(bf16[1024,128]{1,0:T(8,128)(2,1)} %x_ref.1), channel_id=1, source_target_pairs={{0,2},{2,0},{1,3},{3,1},{4,6},{6,4},{5,7},{7,5},{8,10},{10,8},{9,1... | collective-permute-start | bytes 786440 | tf_op jit(solution)/shard_map/ppermute | solution.py:360
  3.0 0.7 %copy-done.17 = s32[1,2,256]{2,1,0:T(2,128)S(1)} copy-done((s32[1,2,256]{2,1,0:T(2,128)S(1)}, s32[1,2,256]{2,1,0:T(2,128)}, u32[]{:S(2)}) %copy-start.17) | copy-done | bytes 2072
  3.7 1.5 %pick_rows.1 = (bf16[256,128]{1,0:T(8,128)(2,1)S(1)}, bf16[256,128]{1,0:T(8,128)(2,1)S(1)}) custom-call(s32[2,256]{1,0:T(2,128)S(1)} %bitcast.6, bf16[1024,128]{1,0:T(8,128)(2,1)} %x_ref.1), custom_call_target="tpu_custom_call" | custom-call | tf_op jit(solution)/shard_map/pick_rows/pallas_call | solution.py:47
  5.1 3.5 %collective-permute-start.3 = (bf16[256,128]{1,0:T(8,128)(2,1)S(1)}, bf16[256,128]{1,0:T(8,128)(2,1)S(1)}, u32[]{:S(2)}, u32[]{:S(2)}) collective-permute-start(bf16[256,128]{1,0:T(8,128)(2,1)S(1)} %get-tuple-element.22), channel_id=1, source_target_pairs={{0,4},{4,8},{8,12},{1,5},{5,9},{9,13},{2,6},{6,10},{10,14},{3,7},{... | collective-permute-start | bytes 196616 | tf_op jit(solution)/shard_map/ppermute | solution.py:397
  8.7 1.3 %collective-permute-start.4 = (bf16[256,128]{1,0:T(8,128)(2,1)S(1)}, bf16[256,128]{1,0:T(8,128)(2,1)S(1)}, u32[]{:S(2)}, u32[]{:S(2)}) collective-permute-start(bf16[256,128]{1,0:T(8,128)(2,1)S(1)} %get-tuple-element.23), channel_id=1, source_target_pairs={{4,0},{8,4},{12,8},{5,1},{9,5},{13,9},{6,2},{10,6},{14,10},{7,3},{... | collective-permute-start | bytes 196616 | tf_op jit(solution)/shard_map/ppermute | solution.py:398
  10.0 0.5 collective-permute-done.3
  10.6 4.5 %collective-permute-done.4 = bf16[256,128]{1,0:T(8,128)(2,1)S(1)} collective-permute-done((bf16[256,128]{1,0:T(8,128)(2,1)S(1)}, bf16[256,128]{1,0:T(8,128)(2,1)S(1)}, u32[]{:S(2)}, u32[]{:S(2)}) %collective-permute-start.4) | collective-permute-done | bytes 65568 | tf_op jit(solution)/shard_map/ppermute | solution.py:398
  15.1 0.6 %collective-permute-start.6 = (bf16[512,128]{1,0:T(8,128)(2,1)S(1)}, bf16[512,128]{1,0:T(8,128)(2,1)S(1)}, u32[]{:S(2)}, u32[]{:S(2)}) collective-permute-start(bf16[512,128]{1,0:T(8,128)(2,1)S(1)} %constant_dynamic-update-slice_fusion.refs_0_), channel_id=1, source_target_pairs={{0,2},{2,0},{1,3},{3,1},{4,6},{6,4},{5,7},{7,5},{8,10},{10,8},{9,1... | collective-permute-start | bytes 393224 | tf_op jit(solution)/shard_map/ppermute | solution.py:360
  15.7 4.5 %collective-permute-done.6.refs_2_ = bf16[512,128]{1,0:T(8,128)(2,1)S(1)} collective-permute-done((bf16[512,128]{1,0:T(8,128)(2,1)S(1)}, bf16[512,128]{1,0:T(8,128)(2,1)S(1)}, u32[]{:S(2)}, u32[]{:S(2)}) %collective-permute-start.6) | collective-permute-done | bytes 131104 | tf_op jit(solution)/shard_map/ppermute | solution.py:360
  20.9 0.2 flip.1
  21.1 0.7 %copy-done.7 = bf16[512,256]{1,0:T(8,128)(2,1)S(1)} copy-done((bf16[512,256]{1,0:T(8,128)(2,1)S(1)}, bf16[512,256]{1,0:T(8,128)(2,1)}, u32[]{:S(2)}) %copy-start.7) | copy-done | bytes 262168
  21.8 2.4 %project.1 = (bf16[256,512]{1,0:T(8,128)(2,1)S(1)}, bf16[1024,256]{1,0:T(8,128)(2,1)S(1)}, bf16[256,1024]{1,0:T(8,128)(2,1)S(1)}, bf16[512,512]{1,0:T(8,128)(2,1)S(1)}) custom-call(s32[1]{0:T(128)} %bitcast.1.chan_ref, s32[1]{0:T(128)} %bitcast.2.sub_ref, bf16[1024,128]{1,0:T(8,128)(2,1)} %x_ref.1, bf16[1024,128]{1,0:T(8,128)(2,1)S(1)} %collective-permute-done.refs_1_, ...), custom_call_target="tpu_custom_call" | custom-call | tf_op jit(solution)/shard_map/project/pallas_call | solution.py:128
  24.3 0.8 %copy-done.5 = bf16[512,512]{1,0:T(8,128)(2,1)} copy-done((bf16[512,512]{1,0:T(8,128)(2,1)}, bf16[512,512]{1,0:T(8,128)(2,1)S(1)}, u32[]{:S(2)}) %copy-start.5) | copy-done | bytes 524312
  25.1 0.9 %extend.1 = (bf16[1536,256]{1,0:T(8,128)(2,1)S(1)}, bf16[256,1536]{1,0:T(8,128)(2,1)S(1)}) custom-call(s32[1]{0:T(128)} %bitcast.1.chan_ref, s32[1]{0:T(128)} %bitcast.2.sub_ref, bf16[512,128]{1,0:T(8,128)(2,1)S(1)} %constant_dynamic-update-slice_fusion.refs_0_, bf16[512,128]{1,0:T(8,128)(2,1)S(1)} %collective-permute-done.5.refs_1_, ...), custom_call_target="tpu_custom_call" | custom-call | tf_op jit(solution)/shard_map/extend/pallas_call | solution.py:165
  26.1 0.6 %copy-done.16 = s32[8,12]{1,0:T(8,128)S(1)} copy-done((s32[8,12]{1,0:T(8,128)S(1)}, s32[8,12]{1,0:T(8,128)}, u32[]{:S(2)}) %copy-start.16) | copy-done | bytes 408
  26.7 4.0 %attend.2.refs_0_ = bf16[256,256]{1,0:T(8,128)(2,1)} custom-call(s32[1]{0:T(128)} %bitcast.2.sub_ref, s32[1]{0:T(128)} %copy.15.live_ref, s32[8,12]{1,0:T(8,128)S(1)} %copy-done.16, bf16[256,512]{1,0:T(8,128)(2,1)S(1)} %get-tuple-element.21.qt_ref, s32[8,12,4,128]{3,2,1,0:T(4,128)S(1)} %copy-done.10, bf16[1536,256]{1,0:T(8,128)(2,1)S(1)} %get-tuple-element.26.k_ref, ...), custom_call_target="tpu_custom_call" | custom-call | tf_op jit(solution)/shard_map/attend/pallas_call | solution.py:290
  30.7 0.5 collective-permute-start.8
  31.2 1.1 %copy-done.3 = bf16[256,1536]{1,0:T(8,128)(2,1)S(1)} copy-done((bf16[256,1536]{1,0:T(8,128)(2,1)S(1)}, bf16[256,1536]{1,0:T(8,128)(2,1)}, u32[]{:S(2)}) %copy-start.3) | copy-done | bytes 786456
  32.4 0.9 %copy-done.9 = bf16[256,512]{1,0:T(8,128)(2,1)S(1)} copy-done((bf16[256,512]{1,0:T(8,128)(2,1)S(1)}, bf16[256,512]{1,0:T(8,128)(2,1)}, u32[]{:S(2)}) %copy-start.9) | copy-done | bytes 262168
  33.3 0.9 %copy-done.11 = s32[8,12,4,128]{3,2,1,0:T(4,128)S(1)} copy-done((s32[8,12,4,128]{3,2,1,0:T(4,128)S(1)}, s32[8,12,4,128]{3,2,1,0:T(4,128)}, u32[]{:S(2)}) %copy-start.11) | copy-done | bytes 196632
  34.3 3.3 %attend.3.refs_0_ = bf16[256,256]{1,0:T(8,128)(2,1)S(1)} custom-call(s32[1]{0:T(128)} %bitcast.2.sub_ref, s32[1]{0:T(128)} %copy.15.live_ref, s32[8,12]{1,0:T(8,128)S(1)} %copy-done.16, bf16[256,512]{1,0:T(8,128)(2,1)S(1)} %copy-done.9, s32[8,12,4,128]{3,2,1,0:T(4,128)S(1)} %copy-done.11, bf16[1536,256]{1,0:T(8,128)(2,1)S(1)} %get-tuple-element.26.k_ref, ...), custom_call_target="tpu_custom_call" | custom-call | tf_op jit(solution)/shard_map/attend/pallas_call | solution.py:290
  37.6 1.6 %collective-permute-start.11 = (bf16[256,256]{1,0:T(8,128)(2,1)S(1)}, bf16[256,256]{1,0:T(8,128)(2,1)}, u32[]{:S(2)}, u32[]{:S(2)}) collective-permute-start(bf16[256,256]{1,0:T(8,128)(2,1)S(1)} %attend.3.refs_0_), channel_id=1, source_target_pairs={{0,2},{2,0},{1,3},{3,1},{4,6},{6,4},{5,7},{7,5},{8,10},{10,8},{9,1... | collective-permute-start | bytes 393224 | tf_op jit(solution)/shard_map/ppermute | solution.py:360
  39.2 1.0 %copy-done.6 = bf16[512,512]{1,0:T(8,128)(2,1)S(1)} copy-done((bf16[512,512]{1,0:T(8,128)(2,1)S(1)}, bf16[512,512]{1,0:T(8,128)(2,1)}, u32[]{:S(2)}) %copy-start.6) | copy-done | bytes 524312
  40.2 2.8 %feed.2 = (bf16[256,256]{1,0:T(8,128)(2,1)}, f32[256,256]{1,0:T(8,128)S(1)}) custom-call(s32[1]{0:T(128)} %bitcast.1.chan_ref, bf16[256,256]{1,0:T(8,128)(2,1)} %attend.2.refs_0_, bf16[256,256]{1,0:T(8,128)(2,1)} %collective-permute-done.8.refs_1_, bf16[512,512]{1,0:T(8,128)(2,1)S(1)} %copy-done.6, bf16[512,512]{1,0:T(8,128)(2,1)S(1)} %copy-done.4, ...), custom_call_target="tpu_custom_call" | custom-call | tf_op jit(solution)/shard_map/feed/pallas_call | solution.py:347
  43.0 0.5 %collective-permute-start.9 = (bf16[256,256]{1,0:T(8,128)(2,1)}, bf16[256,256]{1,0:T(8,128)(2,1)}, u32[]{:S(2)}, u32[]{:S(2)}) collective-permute-start(bf16[256,256]{1,0:T(8,128)(2,1)} %get-tuple-element.30), channel_id=1, source_target_pairs={{0,2},{2,0},{1,3},{3,1},{4,6},{6,4},{5,7},{7,5},{8,10},{10,8},{9,1... | collective-permute-start | bytes 393224 | tf_op jit(solution)/shard_map/ppermute | solution.py:360
  43.6 2.1 %feed.3 = (bf16[256,256]{1,0:T(8,128)(2,1)S(1)}, f32[256,256]{1,0:T(8,128)S(1)}) custom-call(s32[1]{0:T(128)} %bitcast.1.chan_ref, bf16[256,256]{1,0:T(8,128)(2,1)S(1)} %attend.3.refs_0_, bf16[256,256]{1,0:T(8,128)(2,1)} %collective-permute-done.11.refs_1_, bf16[512,512]{1,0:T(8,128)(2,1)S(1)} %copy-done.6, bf16[512,512]{1,0:T(8,128)(2,1)S(1)} %copy-done.4, ...), custom_call_target="tpu_custom_call" | custom-call | tf_op jit(solution)/shard_map/feed/pallas_call | solution.py:347
  45.7 1.6 %collective-permute-start.12 = (bf16[256,256]{1,0:T(8,128)(2,1)S(1)}, bf16[256,256]{1,0:T(8,128)(2,1)S(1)}, u32[]{:S(2)}, u32[]{:S(2)}) collective-permute-start(bf16[256,256]{1,0:T(8,128)(2,1)S(1)} %get-tuple-element.32), channel_id=1, source_target_pairs={{0,2},{2,0},{1,3},{3,1},{4,6},{6,4},{5,7},{7,5},{8,10},{10,8},{9,1... | collective-permute-start | bytes 393224 | tf_op jit(solution)/shard_map/ppermute | solution.py:360
  47.2 2.0 %collective-permute-done.9 = bf16[256,256]{1,0:T(8,128)(2,1)} collective-permute-done((bf16[256,256]{1,0:T(8,128)(2,1)}, bf16[256,256]{1,0:T(8,128)(2,1)}, u32[]{:S(2)}, u32[]{:S(2)}) %collective-permute-start.9) | collective-permute-done | bytes 131104 | tf_op jit(solution)/shard_map/ppermute | solution.py:360
  49.2 1.0 %select_convert_fusion.1 = bf16[256,256]{1,0:T(8,128)(2,1)S(1)} fusion(f32[256,256]{1,0:T(8,128)S(1)} %get-tuple-element.29, bf16[256,256]{1,0:T(8,128)(2,1)} %collective-permute-done.9, pred[256]{0:T(512)(128)(4,1)S(1)} %add_compare_fusion.1), kind=kLoop, calls=%fused_computation.2 | loop fusion | flops 262144 | bytes 524544 | tf_op jit(solution)/shard_map/convert_element_type | solution.py:444
  50.3 1.0 %collective-permute-done.12 = bf16[256,256]{1,0:T(8,128)(2,1)S(1)} collective-permute-done((bf16[256,256]{1,0:T(8,128)(2,1)S(1)}, bf16[256,256]{1,0:T(8,128)(2,1)S(1)}, u32[]{:S(2)}, u32[]{:S(2)}) %collective-permute-start.12) | collective-permute-done | bytes 131104 | tf_op jit(solution)/shard_map/ppermute | solution.py:360
  51.6 1.2 %collective-permute-done.13 = bf16[256,128]{1,0:T(8,128)(2,1)S(1)} collective-permute-done((bf16[256,128]{1,0:T(8,128)(2,1)S(1)}, bf16[256,128]{1,0:T(8,128)(2,1)S(1)}, u32[]{:S(2)}, u32[]{:S(2)}) %collective-permute-start.13) | collective-permute-done | bytes 65568 | tf_op jit(solution)/shard_map/ppermute | solution.py:360
  52.8 0.7 %pad_maximum_fusion = bf16[1024,128]{1,0:T(8,128)(2,1)} fusion(bf16[256,128]{1,0:T(8,128)(2,1)S(1)} %get-tuple-element.36, bf16[256,128]{1,0:T(8,128)(2,1)S(1)} %get-tuple-element.34, bf16[256,128]{1,0:T(8,128)(2,1)S(1)} %get-tuple-element.35, bf16[256,128]{1,0:T(8,128)(2,1)S(1)} %get-tuple-element.33), kind=kLoop, calls=%fused_computation | loop fusion | flops 1048576 | bytes 524288 | tf_op jit(solution)/shard_map/concatenate | solution.py:454
  (51 shorter events, 0.7 us)
Async XLA Ops:
  0.0 10.5 %collective-permute-start.1 = (bf16[1024,128]{1,0:T(8,128)(2,1)}, bf16[1024,128]{1,0:T(8,128)(2,1)S(1)}, u32[]{:S(2)}, u32[]{:S(2)}) collective-permute-start(bf16[1024,128]{1,0:T(8,128)(2,1)} %x_ref.1), channel_id=1, source_target_pairs={{0,2},{2,0},{1,3},{3,1},{4,6},{6,4},{5,7},{7,5},{8,10},{10,8},{9,1... | collective-permute-start | bytes 786440 | tf_op jit(solution)/shard_map/ppermute | solution.py:360
  3.0 0.7 %copy-start.17 = (s32[1,2,256]{2,1,0:T(2,128)S(1)}, s32[1,2,256]{2,1,0:T(2,128)}, u32[]{:S(2)}) copy-start(s32[1,2,256]{2,1,0:T(2,128)} %param.23) | copy-start | bytes 6148
  3.6 17.2 %copy-start.12 = (bf16[512,256]{1,0:T(8,128)(2,1)S(1)}, bf16[512,256]{1,0:T(8,128)(2,1)}, u32[]{:S(2)}) copy-start(bf16[512,256]{1,0:T(8,128)(2,1)} %a_ref.1) | copy-start | bytes 786436
  3.7 17.2 %copy-start.13 = (bf16[512,256]{1,0:T(8,128)(2,1)S(1)}, bf16[512,256]{1,0:T(8,128)(2,1)}, u32[]{:S(2)}) copy-start(bf16[512,256]{1,0:T(8,128)(2,1)} %b_ref.1) | copy-start | bytes 786436
  5.1 5.4 %collective-permute-start.3 = (bf16[256,128]{1,0:T(8,128)(2,1)S(1)}, bf16[256,128]{1,0:T(8,128)(2,1)S(1)}, u32[]{:S(2)}, u32[]{:S(2)}) collective-permute-start(bf16[256,128]{1,0:T(8,128)(2,1)S(1)} %get-tuple-element.22), channel_id=1, source_target_pairs={{0,4},{4,8},{8,12},{1,5},{5,9},{9,13},{2,6},{6,10},{10,14},{3,7},{... | collective-permute-start | bytes 196616 | tf_op jit(solution)/shard_map/ppermute | solution.py:397
  8.6 12.5 %collective-permute-start = (bf16[1024,128]{1,0:T(8,128)(2,1)}, bf16[1024,128]{1,0:T(8,128)(2,1)S(1)}, u32[]{:S(2)}, u32[]{:S(2)}) collective-permute-start(bf16[1024,128]{1,0:T(8,128)(2,1)} %x_ref.1), channel_id=1, source_target_pairs={{0,1},{1,0},{2,3},{3,2},{4,5},{5,4},{6,7},{7,6},{8,9},{9,8},{10,11... | collective-permute-start | bytes 786440 | tf_op jit(solution)/shard_map/ppermute | solution.py:360
  8.7 6.4 %collective-permute-start.4 = (bf16[256,128]{1,0:T(8,128)(2,1)S(1)}, bf16[256,128]{1,0:T(8,128)(2,1)S(1)}, u32[]{:S(2)}, u32[]{:S(2)}) collective-permute-start(bf16[256,128]{1,0:T(8,128)(2,1)S(1)} %get-tuple-element.23), channel_id=1, source_target_pairs={{4,0},{8,4},{12,8},{5,1},{9,5},{13,9},{6,2},{10,6},{14,10},{7,3},{... | collective-permute-start | bytes 196616 | tf_op jit(solution)/shard_map/ppermute | solution.py:398
  10.5 10.6 %collective-permute-start.2 = (bf16[1024,128]{1,0:T(8,128)(2,1)S(1)}, bf16[1024,128]{1,0:T(8,128)(2,1)S(1)}, u32[]{:S(2)}, u32[]{:S(2)}) collective-permute-start(bf16[1024,128]{1,0:T(8,128)(2,1)S(1)} %collective-permute-done.1.refs_2_), channel_id=1, source_target_pairs={{0,1},{1,0},{2,3},{3,2},{4,5},{5,4},{6,7},{7,6},{8,9},{9,8},{10,11... | collective-permute-start | bytes 786440 | tf_op jit(solution)/shard_map/ppermute | solution.py:360
  15.1 5.1 %collective-permute-start.6 = (bf16[512,128]{1,0:T(8,128)(2,1)S(1)}, bf16[512,128]{1,0:T(8,128)(2,1)S(1)}, u32[]{:S(2)}, u32[]{:S(2)}) collective-permute-start(bf16[512,128]{1,0:T(8,128)(2,1)S(1)} %constant_dynamic-update-slice_fusion.refs_0_), channel_id=1, source_target_pairs={{0,2},{2,0},{1,3},{3,1},{4,6},{6,4},{5,7},{7,5},{8,10},{10,8},{9,1... | collective-permute-start | bytes 393224 | tf_op jit(solution)/shard_map/ppermute | solution.py:360
  15.7 9.4 %collective-permute-start.5 = (bf16[512,128]{1,0:T(8,128)(2,1)S(1)}, bf16[512,128]{1,0:T(8,128)(2,1)S(1)}, u32[]{:S(2)}, u32[]{:S(2)}) collective-permute-start(bf16[512,128]{1,0:T(8,128)(2,1)S(1)} %constant_dynamic-update-slice_fusion.refs_0_), channel_id=1, source_target_pairs={{0,1},{1,0},{2,3},{3,2},{4,5},{5,4},{6,7},{7,6},{8,9},{9,8},{10,11... | collective-permute-start | bytes 393224 | tf_op jit(solution)/shard_map/ppermute | solution.py:360
  20.2 4.9 %collective-permute-start.7 = (bf16[512,128]{1,0:T(8,128)(2,1)S(1)}, bf16[512,128]{1,0:T(8,128)(2,1)S(1)}, u32[]{:S(2)}, u32[]{:S(2)}) collective-permute-start(bf16[512,128]{1,0:T(8,128)(2,1)S(1)} %collective-permute-done.6.refs_2_), channel_id=1, source_target_pairs={{0,1},{1,0},{2,3},{3,2},{4,5},{5,4},{6,7},{7,6},{8,9},{9,8},{10,11... | collective-permute-start | bytes 393224 | tf_op jit(solution)/shard_map/ppermute | solution.py:360
  20.9 1.0 %copy-start.7 = (bf16[512,256]{1,0:T(8,128)(2,1)S(1)}, bf16[512,256]{1,0:T(8,128)(2,1)}, u32[]{:S(2)}) copy-start(bf16[512,256]{1,0:T(8,128)(2,1)} %refs_6_.3) | copy-start | bytes 786436
  20.9 0.9 %copy-start.15 = (f32[2,512]{1,0:T(2,128)S(1)}, f32[2,512]{1,0:T(2,128)}, u32[]{:S(2)}) copy-start(f32[2,512]{1,0:T(2,128)} %refs_5_.7) | copy-start | bytes 12292
  21.1 0.7 %copy-start.14 = (f32[2,512]{1,0:T(2,128)S(1)}, f32[2,512]{1,0:T(2,128)}, u32[]{:S(2)}) copy-start(f32[2,512]{1,0:T(2,128)} %refs_4_.7) | copy-start | bytes 12292
  24.3 0.8 %copy-start.5 = (bf16[512,512]{1,0:T(8,128)(2,1)}, bf16[512,512]{1,0:T(8,128)(2,1)S(1)}, u32[]{:S(2)}) copy-start(bf16[512,512]{1,0:T(8,128)(2,1)S(1)} %get-tuple-element.28.refs_2_) | copy-start | bytes 1572868
  25.1 0.9 %copy-start.8 = (bf16[256,512]{1,0:T(8,128)(2,1)}, bf16[256,512]{1,0:T(8,128)(2,1)S(1)}, u32[]{:S(2)}) copy-start(bf16[256,512]{1,0:T(8,128)(2,1)S(1)} %get-tuple-element.21.qt_ref) | copy-start | bytes 786436
  25.1 1.0 %copy-start.10 = (s32[8,12,4,128]{3,2,1,0:T(4,128)S(1)}, s32[8,12,4,128]{3,2,1,0:T(4,128)}, u32[]{:S(2)}) copy-start(s32[8,12,4,128]{3,2,1,0:T(4,128)} %bit_ref.3) | copy-start | bytes 589828
  26.0 4.7 %copy-start.2 = (bf16[256,1536]{1,0:T(8,128)(2,1)}, bf16[256,1536]{1,0:T(8,128)(2,1)S(1)}, u32[]{:S(2)}) copy-start(bf16[256,1536]{1,0:T(8,128)(2,1)S(1)} %get-tuple-element.27.vt_ref) | copy-start | bytes 2359300
  26.0 0.7 %copy-start.16 = (s32[8,12]{1,0:T(8,128)S(1)}, s32[8,12]{1,0:T(8,128)}, u32[]{:S(2)}) copy-start(s32[8,12]{1,0:T(8,128)} %id_ref.3) | copy-start | bytes 1156
  26.7 12.4 %copy-start.4 = (bf16[512,512]{1,0:T(8,128)(2,1)S(1)}, bf16[512,512]{1,0:T(8,128)(2,1)}, u32[]{:S(2)}) copy-start(bf16[512,512]{1,0:T(8,128)(2,1)} %refs_3_.3) | copy-start | bytes 1572868
  30.7 8.4 %collective-permute-start.8 = (bf16[256,256]{1,0:T(8,128)(2,1)}, bf16[256,256]{1,0:T(8,128)(2,1)}, u32[]{:S(2)}, u32[]{:S(2)}) collective-permute-start(bf16[256,256]{1,0:T(8,128)(2,1)} %attend.2.refs_0_), channel_id=1, source_target_pairs={{0,2},{2,0},{1,3},{3,1},{4,6},{6,4},{5,7},{7,5},{8,10},{10,8},{9,1... | collective-permute-start | bytes 393224 | tf_op jit(solution)/shard_map/ppermute | solution.py:360
  31.2 1.1 %copy-start.3 = (bf16[256,1536]{1,0:T(8,128)(2,1)S(1)}, bf16[256,1536]{1,0:T(8,128)(2,1)}, u32[]{:S(2)}) copy-start(bf16[256,1536]{1,0:T(8,128)(2,1)} %copy-done.2) | copy-start | bytes 2359300
  32.4 0.9 %copy-start.9 = (bf16[256,512]{1,0:T(8,128)(2,1)S(1)}, bf16[256,512]{1,0:T(8,128)(2,1)}, u32[]{:S(2)}) copy-start(bf16[256,512]{1,0:T(8,128)(2,1)} %copy-done.8) | copy-start | bytes 786436
  33.3 0.9 %copy-start.11 = (s32[8,12,4,128]{3,2,1,0:T(4,128)S(1)}, s32[8,12,4,128]{3,2,1,0:T(4,128)}, u32[]{:S(2)}) copy-start(s32[8,12,4,128]{3,2,1,0:T(4,128)} %bit_ref.3) | copy-start | bytes 589828
  34.2 4.9 %copy-start = (bf16[1024,512]{1,0:T(8,128)(2,1)S(1)}, bf16[1024,512]{1,0:T(8,128)(2,1)}, u32[]{:S(2)}) copy-start(bf16[1024,512]{1,0:T(8,128)(2,1)} %refs_6_.5) | copy-start | bytes 3145732
  34.2 4.9 %copy-start.1 = (bf16[1024,512]{1,0:T(8,128)(2,1)S(1)}, bf16[1024,512]{1,0:T(8,128)(2,1)}, u32[]{:S(2)}) copy-start(bf16[1024,512]{1,0:T(8,128)(2,1)} %refs_7_.5) | copy-start | bytes 3145732
  37.6 6.0 %collective-permute-start.11 = (bf16[256,256]{1,0:T(8,128)(2,1)S(1)}, bf16[256,256]{1,0:T(8,128)(2,1)}, u32[]{:S(2)}, u32[]{:S(2)}) collective-permute-start(bf16[256,256]{1,0:T(8,128)(2,1)S(1)} %attend.3.refs_0_), channel_id=1, source_target_pairs={{0,2},{2,0},{1,3},{3,1},{4,6},{6,4},{5,7},{7,5},{8,10},{10,8},{9,1... | collective-permute-start | bytes 393224 | tf_op jit(solution)/shard_map/ppermute | solution.py:360
  39.1 1.0 %copy-start.6 = (bf16[512,512]{1,0:T(8,128)(2,1)S(1)}, bf16[512,512]{1,0:T(8,128)(2,1)}, u32[]{:S(2)}) copy-start(bf16[512,512]{1,0:T(8,128)(2,1)} %copy-done.5) | copy-start | bytes 1572868
  43.0 6.2 %collective-permute-start.9 = (bf16[256,256]{1,0:T(8,128)(2,1)}, bf16[256,256]{1,0:T(8,128)(2,1)}, u32[]{:S(2)}, u32[]{:S(2)}) collective-permute-start(bf16[256,256]{1,0:T(8,128)(2,1)} %get-tuple-element.30), channel_id=1, source_target_pairs={{0,2},{2,0},{1,3},{3,1},{4,6},{6,4},{5,7},{7,5},{8,10},{10,8},{9,1... | collective-permute-start | bytes 393224 | tf_op jit(solution)/shard_map/ppermute | solution.py:360
  45.7 5.7 %collective-permute-start.12 = (bf16[256,256]{1,0:T(8,128)(2,1)S(1)}, bf16[256,256]{1,0:T(8,128)(2,1)S(1)}, u32[]{:S(2)}, u32[]{:S(2)}) collective-permute-start(bf16[256,256]{1,0:T(8,128)(2,1)S(1)} %get-tuple-element.32), channel_id=1, source_target_pairs={{0,2},{2,0},{1,3},{3,1},{4,6},{6,4},{5,7},{7,5},{8,10},{10,8},{9,1... | collective-permute-start | bytes 393224 | tf_op jit(solution)/shard_map/ppermute | solution.py:360
  50.3 1.3 %collective-permute-start.10 = (bf16[256,128]{1,0:T(8,128)(2,1)S(1)}, bf16[256,128]{1,0:T(8,128)(2,1)S(1)}, u32[]{:S(2)}, u32[]{:S(2)}) collective-permute-start(bf16[256,128]{1,0:T(8,128)(2,1)S(1)} %broadcast_select_fusion.6), channel_id=1, source_target_pairs={{0,1},{1,0},{2,3},{3,2},{4,5},{5,4},{6,7},{7,6},{8,9},{9,8},{10,11... | collective-permute-start | bytes 196616 | tf_op jit(solution)/shard_map/ppermute | solution.py:360
  51.5 1.3 %collective-permute-start.13 = (bf16[256,128]{1,0:T(8,128)(2,1)S(1)}, bf16[256,128]{1,0:T(8,128)(2,1)S(1)}, u32[]{:S(2)}, u32[]{:S(2)}) collective-permute-start(bf16[256,128]{1,0:T(8,128)(2,1)S(1)} %broadcast_select_fusion.3), channel_id=1, source_target_pairs={{0,1},{1,0},{2,3},{3,2},{4,5},{5,4},{6,7},{7,6},{8,9},{9,8},{10,11... | collective-permute-start | bytes 196616 | tf_op jit(solution)/shard_map/ppermute | solution.py:360
